TPU v7x, 512 devices: a whole 4x8x8 slice. The times are simulated.
512 devices in a mesh: dp: 32 (over y, x), mp: 16 (over z, core).
Axes of the slice: x: 4, y: 8, z: 8, core: 2. Of those that a mesh axis runs over, the one named last changes fastest.
Arguments:
- query_new: bfloat16 [512, 4096], P(('dp', 'mp')), parts along dimension 0, may hold values from -140 to 140
- key_new: bfloat16 [512, 1024], P(('dp', 'mp')), parts along dimension 0, may hold values from -5 to 5
- value_new: bfloat16 [512, 1024], P(('dp', 'mp')), parts along dimension 0, may hold values from -5 to 5
- prefix_keys: bfloat16 [65536, 1024], P(('dp', 'mp')), parts along dimension 0, may hold values from -5 to 5
- prefix_values: bfloat16 [65536, 1024], P(('dp', 'mp')), parts along dimension 0, may hold values from -5 to 5
- sample_suffix_keys: bfloat16 [512, 64, 1024], P(('dp', 'mp')), parts along dimension 0, may hold values from -5 to 5
- sample_suffix_values: bfloat16 [512, 64, 1024], P(('dp', 'mp')), parts along dimension 0, may hold values from -5 to 5
- prefix_len: int32 [32], P('dp'), parts along dimension 0, may hold values from 512 to 2048
- suffix_len: int32 [512], P(('dp', 'mp')), parts along dimension 0, may hold values from 1 to 64, as said below
- residual: bfloat16 [512, 8192], P(('dp', 'mp')), parts along dimension 0, may hold values from -3 to 3
- out_weight: bfloat16 [4096, 8192], P('mp'), may hold values from -0.1875 to 0.1875
- norm_gain: bfloat16 [8192], replicated, may hold values from 0.5 to 1.5
Outputs:
- hidden: bfloat16 [512, 8192], P(('dp', 'mp')), parts along dimension 0
- normed: bfloat16 [512, 8192], P(('dp', 'mp')), parts along dimension 0
There are 32 independent parts, one for each index of `dp`. A program takes and returns all parts, laid end to end along the dimension named above; an argument that names none is the same for every part. Nothing has to cross between parts.
Inputs may be any that keep to these rules, and one draw needn't show every extreme that they name: `suffix_len`: some sample has exactly 64 cached generated tokens.
All inputs are finite; a program needn't handle non-finite values.
Results may differ from a plain program's by a relative error of at most 0.0085.
Values may be sent and summed in bfloat16 or wider, within the bound.
No kernel may reach another device: no remote copies, remote signals or barrier semaphores. Data moves between devices by JAX's collectives and lax.ppermute only.
A program may use at most 64 MiB of HBM per device.

v0:
```python
import jax
import jax.numpy as jnp
from jax import lax
from jax.experimental import pallas as pl
from jax.experimental.pallas import tpu as pltpu
from jax.sharding import PartitionSpec as P


HEAD_SIZE = 128
KEY_VALUE_HEADS = 8
HQ = 32
GROUP = HQ // KEY_VALUE_HEADS
SAMPLES = 16
CHIPS = 8
D = 8192
BLOCKS = D // 128
WIDTH = 1024
ROWS = 40
SCALE = HEAD_SIZE ** (-0.5)
MASKED = -1e30
LOWEST = -1e29
F32 = jnp.float32
BF16 = jnp.bfloat16

LONG = pl.CostEstimate(flops=10**10, bytes_accessed=10**6, transcendentals=0)


def vmem(count):
    return [pl.BlockSpec(memory_space=pltpu.VMEM)] * count


def at_most(mebibytes):
    return pltpu.CompilerParams(vmem_limit_bytes=mebibytes * 2**20)


def smem(count):
    return [pl.BlockSpec(memory_space=pltpu.SMEM)] * count


def spread_kernel(query_ref, out_ref):
    rows = [query_ref[0:1, h * 128 : (h + 1) * 128].astype(F32) for h in range(HQ)]
    rows = jnp.concatenate(rows, axis=0).astype(BF16)
    for i in range(SAMPLES):
        out_ref[i] = rows


def attend_kernel(
    place_ref,
    prefix_len_ref,
    suffix_len_ref,
    query_ref,
    pkeys_ref,
    pvalues_ref,
    skeys_ref,
    svalues_ref,
    key_ref,
    value_ref,
    out_ref,
    queries,
):
    place = place_ref[0]
    queries[...] = query_ref[...].reshape(SAMPLES * HQ, 128).astype(F32)
    row = lax.broadcasted_iota(jnp.int32, (64, 128), 0)
    lane = lax.broadcasted_iota(jnp.int32, (64, 128), 1)
    sample = 2 * (row % 8) + row // 32
    prefix_seen = lane + place * 128 < prefix_len_ref[0]
    own_seen = (sample == place) & ((lane < suffix_len_ref[0]) | (lane == 64))
    first = row == 0
    mark = lane[:32] == row[:32] + 32 * (place % 4)
    ones = jnp.ones((256, 128), BF16)
    zeros = jnp.zeros((5, 128), F32)
    for k in range(KEY_VALUE_HEADS):
        head = slice(k * 128, (k + 1) * 128)
        new_key = jnp.where(first, key_ref[0:1, head].astype(F32), 0.0).astype(BF16)
        new_value = jnp.where(first, value_ref[0:1, head].astype(F32), 0.0).astype(BF16)
        keys = jnp.concatenate([pkeys_ref[:, head], skeys_ref[0, :, head], new_key], axis=0)
        values = jnp.concatenate([pvalues_ref[:, head], svalues_ref[0, :, head], new_value], axis=0)
        query = [
            queries[pl.ds(c * HQ + k * GROUP + g, 8, stride=2 * HQ), :]
            for c in range(2)
            for g in range(GROUP)
        ]
        query = jnp.concatenate(query, axis=0).astype(BF16)
        scores = lax.dot_general(
            query, keys, (((1,), (1,)), ((), ())), preferred_element_type=F32
        )
        s_pre = jnp.where(prefix_seen, scores[:, :128] * SCALE, MASKED)
        s_own = jnp.where(own_seen, scores[:, 128:] * SCALE, MASKED)
        top = jnp.max(jnp.maximum(s_pre, s_own), axis=-1, keepdims=True)
        top = jnp.maximum(top, LOWEST).astype(BF16).astype(F32)
        weights = jnp.concatenate([jnp.exp(s_pre - top), jnp.exp(s_own - top)], axis=1)
        summed = jnp.dot(
            weights.astype(BF16),
            jnp.concatenate([values, ones], axis=1),
            preferred_element_type=F32,
        )
        total = summed[:, 128:]
        total_high = total.astype(BF16).astype(F32)
        total_low = total - total_high
        for c in range(2):
            part = slice(32 * c, 32 * c + 32)
            out_ref[2 * k + c, 0:32, :] = summed[part, :128].astype(BF16)
            stats = [
                jnp.sum(jnp.where(mark, v[part], 0.0), axis=0, keepdims=True)
                for v in (top, total_high, total_low)
            ]
            out_ref[2 * k + c, 32:ROWS, :] = jnp.concatenate(stats + [zeros], axis=0).astype(BF16)


def project_kernel(place_ref, got_ref, own_ref, other_hbm, out_ref, rows, other_ref, arrived):
    copies = [
        pltpu.make_async_copy(
            other_hbm.at[:, n : n + WIDTH], other_ref.at[:, n : n + WIDTH], arrived.at[n // WIDTH]
        )
        for n in range(0, D, WIDTH)
    ]
    for copy in copies:
        copy.start()
    stats = got_ref[:, 32:ROWS, :].astype(F32)
    quads = [
        stats[4 * q] + stats[4 * q + 1] + stats[4 * q + 2] + stats[4 * q + 3] for q in range(4)
    ]
    tops = [s[0:1] for s in quads]
    totals = [s[1:2] + s[2:3] for s in quads]
    top = jnp.maximum(jnp.maximum(tops[0], tops[1]), jnp.maximum(tops[2], tops[3]))
    top = jnp.maximum(top, pltpu.roll(top, 64, 1))
    top = jnp.maximum(top, pltpu.roll(top, 32, 1))
    factors = [jnp.exp(t - top) for t in tops]
    total = sum(f * t for f, t in zip(factors, totals))
    total = total + pltpu.roll(total, 64, 1)
    total = total + pltpu.roll(total, 32, 1)
    row = lax.broadcasted_iota(jnp.int32, (32, 128), 0)
    lane = lax.broadcasted_iota(jnp.int32, (32, 128), 1)
    diagonal = lane % 32 == row
    mix = jnp.concatenate([jnp.where(diagonal, f / total, 0.0) for f in factors], axis=1)
    high = mix.astype(BF16)
    low = (mix - high.astype(F32)).astype(BF16)
    sums = got_ref[:, 0:32, :].reshape(SAMPLES * 32, 128)
    both = jnp.dot(jnp.concatenate([high, low], axis=0), sums, preferred_element_type=F32)
    attn = both[:32] + both[32:]
    attn = jnp.concatenate([attn[8 * g : 8 * g + 8] for g in range(GROUP)], axis=1)
    north = place_ref[0] % 2 == 1
    mine = jnp.where(north, attn[:, 256:], attn[:, :256]).astype(BF16)
    others = jnp.where(north, attn[:, :256], attn[:, 256:]).astype(BF16)
    for n in range(0, D, WIDTH):
        cols = slice(n, n + WIDTH)
        piece = jnp.dot(mine, own_ref[:, cols], preferred_element_type=F32)
        copies[n // WIDTH].wait()
        piece += jnp.dot(others, other_ref[:, cols], preferred_element_type=F32)
        for i in range(WIDTH // 128):
            rows[pl.ds(n // 128 + i, 8, stride=BLOCKS), :] = piece[:, 128 * i : 128 * i + 128]
    out_ref[...] = rows[...].astype(BF16).reshape(CHIPS, BLOCKS, 128)


def stage_kernel(residual_ref, gain_ref, residual_rows_ref, gain_rows_ref):
    rows = [residual_ref[0:1, 128 * i : 128 * i + 128].astype(F32) for i in range(BLOCKS)]
    residual_rows_ref[...] = jnp.concatenate(rows, axis=0)
    gain_rows_ref[...] = gain_ref[...].astype(F32)


def finish_kernel(got_ref, residual_ref, gain_ref, hidden_ref, normed_ref):
    proj = got_ref[0].astype(F32)
    for i in range(1, CHIPS):
        proj += got_ref[i].astype(F32)
    stream = residual_ref[...] + proj
    scale = lax.rsqrt(jnp.sum(stream * stream) * (1.0 / D) + 1e-05)
    normed = stream * scale * gain_ref[...]
    for i in range(BLOCKS):
        cols = slice(128 * i, 128 * i + 128)
        hidden_ref[0:1, cols] = stream[i : i + 1].astype(BF16)
        normed_ref[0:1, cols] = normed[i : i + 1].astype(BF16)


def local(
    query_new,
    key_new,
    value_new,
    prefix_keys,
    prefix_values,
    sample_suffix_keys,
    sample_suffix_values,
    prefix_len,
    suffix_len,
    residual,
    out_weight,
    norm_gain,
):
    place = lax.axis_index("mp").astype(jnp.int32)[None]
    cores = [[2 * z + c for z in range(CHIPS)] for c in range(2)]
    other_weight = lax.ppermute(out_weight, "mp", [(i, i ^ 1) for i in range(SAMPLES)])
    spread = pl.pallas_call(
        spread_kernel,
        out_shape=jax.ShapeDtypeStruct((SAMPLES, HQ, 128), BF16),
        in_specs=vmem(1),
        out_specs=vmem(1)[0],
        compiler_params=at_most(2),
        cost_estimate=LONG,
    )(query_new)
    queries = lax.all_to_all(spread, "mp", 0, 0, tiled=True)
    residual_rows, gain_rows = pl.pallas_call(
        stage_kernel,
        out_shape=[jax.ShapeDtypeStruct((BLOCKS, 128), F32)] * 2,
        in_specs=vmem(2),
        out_specs=vmem(2),
        compiler_params=at_most(2),
        cost_estimate=LONG,
    )(residual, norm_gain.reshape(BLOCKS, 128))
    partial = pl.pallas_call(
        attend_kernel,
        out_shape=jax.ShapeDtypeStruct((SAMPLES, ROWS, 128), BF16),
        in_specs=smem(3) + vmem(7),
        out_specs=vmem(1)[0],
        scratch_shapes=[pltpu.VMEM((SAMPLES * HQ, 128), F32)],
        compiler_params=at_most(8),
        cost_estimate=LONG,
    )(
        place,
        prefix_len,
        suffix_len,
        queries,
        prefix_keys,
        prefix_values,
        sample_suffix_keys,
        sample_suffix_values,
        key_new,
        value_new,
    )
    partial = lax.all_to_all(partial, "mp", 0, 0, tiled=True)
    proj = pl.pallas_call(
        project_kernel,
        out_shape=jax.ShapeDtypeStruct((CHIPS, BLOCKS, 128), BF16),
        in_specs=smem(1) + vmem(2) + [pl.BlockSpec(memory_space=pl.ANY)],
        out_specs=vmem(1)[0],
        scratch_shapes=[
            pltpu.VMEM((8 * BLOCKS, 128), F32),
            pltpu.VMEM((256, D), BF16),
            pltpu.SemaphoreType.DMA((D // WIDTH,)),
        ],
        compiler_params=at_most(16),
        cost_estimate=LONG,
    )(place, partial, out_weight, other_weight)
    proj = lax.all_to_all(proj, "mp", 0, 0, tiled=True, axis_index_groups=cores)
    return tuple(
        pl.pallas_call(
            finish_kernel,
            out_shape=[jax.ShapeDtypeStruct((1, D), BF16)] * 2,
            in_specs=vmem(3),
            out_specs=vmem(2),
            compiler_params=at_most(4),
        )(proj, residual_rows, gain_rows)
    )


def solution(mesh):
    whole = P(("dp", "mp"), None)
    placed = (
        whole,
        whole,
        whole,
        whole,
        whole,
        P(("dp", "mp"), None, None),
        P(("dp", "mp"), None, None),
        P("dp"),
        P(("dp", "mp")),
        whole,
        P("mp", None),
        P(),
    )

    def step(*arrays):
        return local(*arrays)

    step = jax.shard_map(
        step, mesh=mesh, in_specs=placed, out_specs=(whole, whole), check_vma=False
    )
    return step
```

profile of v0, /device:TPU:1, one launch (start us, length us, event | category | flops | bytes accessed | tf_op | source)
XLA Modules:
  0.0 57.4 jit_solution(6435718654641194500)
XLA Ops:
  0.6 0.0 copy-start.1
  0.6 0.0 copy-start.2
  0.7 0.0 copy-start.3
  0.7 0.0 copy-start.4
  0.7 8.9 %collective-permute-start = (bf16[256,8192]{1,0:T(8,128)(2,1)}, bf16[256,8192]{1,0:T(8,128)(2,1)}, u32[]{:S(2)}, u32[]{:S(2)}) collective-permute-start(bf16[256,8192]{1,0:T(8,128)(2,1)} %own_ref.1), channel_id=1, source_target_pairs={{0,1},{1,0},{2,3},{3,2},{4,5},{5,4},{6,7},{7,6},{8,9},{9,8},{10,11... | collective-permute-start | bytes 12582920 | tf_op jit(solution)/shard_map/ppermute | solution.py:190
  9.6 0.0 copy-start.6
  9.6 0.7 %copy-done.6 = bf16[1,4096]{1,0:T(2,128)(2,1)S(1)} copy-done((bf16[1,4096]{1,0:T(2,128)(2,1)S(1)}, bf16[1,4096]{1,0:T(2,128)(2,1)}, u32[]{:S(2)}) %copy-start.6) | copy-done | bytes 8216
  10.3 0.0 copy-start.8
  10.3 0.0 copy-start.9
  10.3 0.7 %shard_map.131 = bf16[16,32,128]{2,1,0:T(8,128)(2,1)} custom-call(bf16[1,4096]{1,0:T(2,128)(2,1)S(1)} %copy-done.6), custom_call_target="tpu_custom_call" | custom-call | flops 10000000000 | bytes 1000000 | tf_op jit(solution)/shard_map/pallas_call | solution.py:191
  11.0 5.1 %all-to-all-start = ((bf16[16,32,128]{2,1,0:T(8,128)(2,1)}), bf16[16,32,128]{2,1,0:T(8,128)(2,1)S(1)}, u32[]{:S(2)}, u32[]{:S(2)}) async-start(bf16[16,32,128]{2,1,0:T(8,128)(2,1)} %shard_map.131), calls=%async_computation | async-start | bytes 262144 | tf_op jit(solution)/shard_map/all_to_all | solution.py:199
  17.3 7.6 %all-to-all-done.query_ref = bf16[16,32,128]{2,1,0:T(8,128)(2,1)S(1)} async-done(((bf16[16,32,128]{2,1,0:T(8,128)(2,1)}), bf16[16,32,128]{2,1,0:T(8,128)(2,1)S(1)}, u32[]{:S(2)}, u32[]{:S(2)}) %all-to-all-start) | async-done | bytes 131104 | tf_op jit(solution)/shard_map/all_to_all | solution.py:199
  24.9 0.0 copy-done.1
  24.9 0.0 copy-done.2
  24.9 0.0 copy-done.3
  24.9 0.0 copy-done.4
  25.0 0.0 copy-done.8
  25.0 0.0 copy-done.9
  25.0 0.0 copy-start
  25.0 2.3 %shard_map.132 = bf16[16,40,128]{2,1,0:T(8,128)(2,1)S(1)} custom-call(s32[1]{0:T(128)} %bitcast.place_ref, s32[1]{0:T(128)S(6)} %copy.14.prefix_len_ref, s32[1]{0:T(128)S(6)} %copy.15.suffix_len_ref, bf16[16,32,128]{2,1,0:T(8,128)(2,1)S(1)} %all-to-all-done.query_ref, bf16[128,1024]{1,0:T(8,128)(2,1)S(1)} %copy-done.1, bf16[128,1024]{1,0:T(8,128)(2,1)S(1)} %copy-done.2, ...), custom_call_target="tpu_custom_call" | custom-call | flops 10000000000 | bytes 1000000 | tf_op jit(solution)/shard_map/pallas_call | solution.py:208
  27.3 12.2 %all_to_all.15.got_ref = bf16[16,40,128]{2,1,0:T(8,128)(2,1)S(1)} all-to-all(bf16[16,40,128]{2,1,0:T(8,128)(2,1)S(1)} %shard_map.132), channel_id=1, replica_groups=mesh['dp'=32,'mp'=16] {'mp'}, dimensions={0} | all-to-all | bytes 327680 | tf_op jit(solution)/shard_map/all_to_all | solution.py:228
  39.5 0.0 copy-start.5
  39.5 0.0 copy-start.7
  39.5 0.0 collective-permute-done.other_hbm
  39.5 0.0 copy-done
  39.5 4.2 %shard_map.133 = bf16[8,64,128]{2,1,0:T(8,128)(2,1)} custom-call(s32[1]{0:T(128)} %bitcast.place_ref, bf16[16,40,128]{2,1,0:T(8,128)(2,1)S(1)} %all_to_all.15.got_ref, bf16[256,8192]{1,0:T(8,128)(2,1)S(1)} %copy-done, bf16[256,8192]{1,0:T(8,128)(2,1)} %collective-permute-done.other_hbm), custom_call_target="tpu_custom_call" | custom-call | flops 10000000000 | bytes 1000000 | tf_op jit(solution)/shard_map/pallas_call | solution.py:229
  43.6 3.4 %all-to-all-start.2 = ((bf16[8,64,128]{2,1,0:T(8,128)(2,1)}), bf16[8,64,128]{2,1,0:T(8,128)(2,1)S(1)}, u32[]{:S(2)}, u32[]{:S(2)}) async-start(bf16[8,64,128]{2,1,0:T(8,128)(2,1)} %shard_map.133), calls=%async_computation.2 | async-start | bytes 262144 | tf_op jit(solution)/shard_map/all_to_all | solution.py:242
  47.0 0.0 copy-done.5
  47.0 0.0 copy-done.7
  47.1 9.5 %all-to-all-done.2.got_ref = bf16[8,64,128]{2,1,0:T(8,128)(2,1)S(1)} async-done(((bf16[8,64,128]{2,1,0:T(8,128)(2,1)}), bf16[8,64,128]{2,1,0:T(8,128)(2,1)S(1)}, u32[]{:S(2)}, u32[]{:S(2)}) %all-to-all-start.2) | async-done | bytes 131104 | tf_op jit(solution)/shard_map/all_to_all | solution.py:242
  56.5 0.8 %shard_map.135 = (bf16[1,8192]{1,0:T(2,128)(2,1)}, bf16[1,8192]{1,0:T(2,128)(2,1)}) custom-call(bf16[8,64,128]{2,1,0:T(8,128)(2,1)S(1)} %all-to-all-done.2.got_ref, f32[64,128]{1,0:T(8,128)S(1)} %get-tuple-element.4.residual_ref, f32[64,128]{1,0:T(8,128)S(1)} %get-tuple-element.5.gain_ref), custom_call_target="tpu_custom_call" | custom-call | tf_op jit(solution)/shard_map/pallas_call | solution.py:244
  (1 shorter events, 0.0 us)
Async XLA Ops:
  0.6 24.3 %copy-start.1 = (bf16[128,1024]{1,0:T(8,128)(2,1)S(1)}, bf16[128,1024]{1,0:T(8,128)(2,1)}, u32[]{:S(2)}) copy-start(bf16[128,1024]{1,0:T(8,128)(2,1)} %pkeys_ref.1) | copy-start | bytes 786436
  0.6 24.3 %copy-start.2 = (bf16[128,1024]{1,0:T(8,128)(2,1)S(1)}, bf16[128,1024]{1,0:T(8,128)(2,1)}, u32[]{:S(2)}) copy-start(bf16[128,1024]{1,0:T(8,128)(2,1)} %pvalues_ref.1) | copy-start | bytes 786436
  0.7 24.3 %copy-start.3 = (bf16[1,64,1024]{2,1,0:T(8,128)(2,1)S(1)}, bf16[1,64,1024]{2,1,0:T(8,128)(2,1)}, u32[]{:S(2)}) copy-start(bf16[1,64,1024]{2,1,0:T(8,128)(2,1)} %skeys_ref.1) | copy-start | bytes 393220
  0.7 24.3 %copy-start.4 = (bf16[1,64,1024]{2,1,0:T(8,128)(2,1)S(1)}, bf16[1,64,1024]{2,1,0:T(8,128)(2,1)}, u32[]{:S(2)}) copy-start(bf16[1,64,1024]{2,1,0:T(8,128)(2,1)} %svalues_ref.1) | copy-start | bytes 393220
  0.7 38.8 %collective-permute-start = (bf16[256,8192]{1,0:T(8,128)(2,1)}, bf16[256,8192]{1,0:T(8,128)(2,1)}, u32[]{:S(2)}, u32[]{:S(2)}) collective-permute-start(bf16[256,8192]{1,0:T(8,128)(2,1)} %own_ref.1), channel_id=1, source_target_pairs={{0,1},{1,0},{2,3},{3,2},{4,5},{5,4},{6,7},{7,6},{8,9},{9,8},{10,11... | collective-permute-start | bytes 12582920 | tf_op jit(solution)/shard_map/ppermute | solution.py:190
  9.6 0.7 %copy-start.6 = (bf16[1,4096]{1,0:T(2,128)(2,1)S(1)}, bf16[1,4096]{1,0:T(2,128)(2,1)}, u32[]{:S(2)}) copy-start(bf16[1,4096]{1,0:T(2,128)(2,1)} %query_ref.1) | copy-start | bytes 24580
  10.3 14.7 %copy-start.8 = (bf16[1,1024]{1,0:T(2,128)(2,1)S(1)}, bf16[1,1024]{1,0:T(2,128)(2,1)}, u32[]{:S(2)}) copy-start(bf16[1,1024]{1,0:T(2,128)(2,1)} %key_ref.1) | copy-start | bytes 6148
  10.3 14.7 %copy-start.9 = (bf16[1,1024]{1,0:T(2,128)(2,1)S(1)}, bf16[1,1024]{1,0:T(2,128)(2,1)}, u32[]{:S(2)}) copy-start(bf16[1,1024]{1,0:T(2,128)(2,1)} %value_ref.1) | copy-start | bytes 6148
  11.0 14.0 %all-to-all-start = ((bf16[16,32,128]{2,1,0:T(8,128)(2,1)}), bf16[16,32,128]{2,1,0:T(8,128)(2,1)S(1)}, u32[]{:S(2)}, u32[]{:S(2)}) async-start(bf16[16,32,128]{2,1,0:T(8,128)(2,1)} %shard_map.131), calls=%async_computation | async-start | bytes 262144 | tf_op jit(solution)/shard_map/all_to_all | solution.py:199
  25.0 14.5 %copy-start = (bf16[256,8192]{1,0:T(8,128)(2,1)S(1)}, bf16[256,8192]{1,0:T(8,128)(2,1)}, u32[]{:S(2)}) copy-start(bf16[256,8192]{1,0:T(8,128)(2,1)} %own_ref.1) | copy-start | bytes 12582916
  39.5 7.6 %copy-start.5 = (bf16[1,8192]{1,0:T(2,128)(2,1)S(1)}, bf16[1,8192]{1,0:T(2,128)(2,1)}, u32[]{:S(2)}) copy-start(bf16[1,8192]{1,0:T(2,128)(2,1)} %residual_ref.1) | copy-start | bytes 49156
  39.5 7.6 %copy-start.7 = (bf16[8192]{0:T(1024)(128)(2,1)S(1)}, bf16[8192]{0:T(1024)(128)(2,1)}, u32[]{:S(2)}) copy-start(bf16[8192]{0:T(1024)(128)(2,1)} %param.23) | copy-start | bytes 49156
  43.6 12.9 %all-to-all-start.2 = ((bf16[8,64,128]{2,1,0:T(8,128)(2,1)}), bf16[8,64,128]{2,1,0:T(8,128)(2,1)S(1)}, u32[]{:S(2)}, u32[]{:S(2)}) async-start(bf16[8,64,128]{2,1,0:T(8,128)(2,1)} %shard_map.133), calls=%async_computation.2 | async-start | bytes 262144 | tf_op jit(solution)/shard_map/all_to_all | solution.py:242
where the time goes:
time: 57.8 us; the launch traced here: 57.4 us
  starting transfers between devices  17.4 us (30%)
  waiting for transfers between devices  17.1 us (30%)
  blocking collectives  12.2 us (21%)
  Pallas kernels  7.94 us (14%)
  between operations  2.07 us (4%)
  local copies, waits for them, and re-layouts  0.75 us (1%)
    all_to_all x1, blocking collectives, local(): partial = lax.all_to_all(partial, 'mp', 0, 0, tiled=True)  12.2 us
    all_to_all x1, waiting for transfers between devices, local(): proj = lax.all_to_all(proj, 'mp', 0, 0, tiled=True, axis_index_groups=cores)  9.46 us
    ppermute x1, starting transfers between devices, local(): lax.ppermute(out_weight, 'mp', [(i, i ^ 1) for i in range(SAMPLES)])  8.88 us
    all_to_all x1, waiting for transfers between devices, local(): queries = lax.all_to_all(spread, 'mp', 0, 0, tiled=True)  7.59 us
    all_to_all x1, starting transfers between devices, local(): queries = lax.all_to_all(spread, 'mp', 0, 0, tiled=True)  5.1 us
    pallas_call x1, Pallas kernels, local(): pl.pallas_call(project_kernel, out_shape=jax.ShapeDtypeStruct((CHIPS, BLO...  4.15 us
    all_to_all x1, starting transfers between devices, local(): proj = lax.all_to_all(proj, 'mp', 0, 0, tiled=True, axis_index_groups=cores)  3.38 us
    pallas_call x1, Pallas kernels, local(): pl.pallas_call(attend_kernel, out_shape=jax.ShapeDtypeStruct((SAMPLES, RO...  2.26 us
  transfers between devices with their start and end apart: 3, of which 2 were waited for; matrix products, arithmetic and copies ran while one was open for 0% of the time, Pallas kernels for 5%

commit v1 on v0

v1 whole, which is shorter than its diff:
```python
import jax
import jax.numpy as jnp
from jax import lax
from jax.experimental import pallas as pl
from jax.experimental.pallas import tpu as pltpu
from jax.sharding import PartitionSpec as P


HEAD_SIZE = 128
KEY_VALUE_HEADS = 8
HQ = 32
GROUP = HQ // KEY_VALUE_HEADS
SAMPLES = 16
CHIPS = 8
D = 8192
BLOCKS = D // 128
WIDTH = 1024
ROWS = 40
SCALE = HEAD_SIZE ** (-0.5)
MASKED = -1e30
LOWEST = -1e29
F32 = jnp.float32
BF16 = jnp.bfloat16

LONG = pl.CostEstimate(flops=10**10, bytes_accessed=10**6, transcendentals=0)


def vmem(count):
    return [pl.BlockSpec(memory_space=pltpu.VMEM)] * count


def hbm(count):
    return [pl.BlockSpec(memory_space=pltpu.HBM)] * count


def at_most(mebibytes):
    return pltpu.CompilerParams(vmem_limit_bytes=mebibytes * 2**20)


def smem(count):
    return [pl.BlockSpec(memory_space=pltpu.SMEM)] * count


def spread_kernel(query_ref, out_ref):
    rows = [query_ref[0:1, h * 128 : (h + 1) * 128].astype(F32) for h in range(HQ)]
    rows = jnp.concatenate(rows, axis=0).astype(BF16)
    for i in range(CHIPS):
        out_ref[i] = rows


def stage_kernel(
    place_ref,
    prefix_len_hbm,
    suffix_len_hbm,
    pkeys_ref,
    pvalues_ref,
    skeys_ref,
    svalues_ref,
    key_ref,
    value_ref,
    residual_ref,
    gain_ref,
    prefix_ref,
    own_ref,
    bias_ref,
    residual_rows_ref,
    gain_rows_ref,
    lengths,
    arrived,
):
    copies = [
        pltpu.make_async_copy(source, lengths.at[i], arrived.at[i])
        for i, source in enumerate((prefix_len_hbm, suffix_len_hbm))
    ]
    for copy in copies:
        copy.start()
    prefix_ref[:128] = pkeys_ref[...]
    prefix_ref[128:] = pvalues_ref[...]
    first = lax.broadcasted_iota(jnp.int32, (64, 1024), 0) == 0
    own_ref[0:64] = skeys_ref[0]
    own_ref[64:128] = jnp.where(first, key_ref[...].astype(F32), 0.0).astype(BF16)
    own_ref[128:192] = svalues_ref[0]
    own_ref[192:256] = jnp.where(first, value_ref[...].astype(F32), 0.0).astype(BF16)
    rows = [residual_ref[0:1, 128 * i : 128 * i + 128].astype(F32) for i in range(BLOCKS)]
    residual_rows_ref[...] = jnp.concatenate(rows, axis=0)
    gain_rows_ref[...] = gain_ref[...].astype(F32)
    for copy in copies:
        copy.wait()
    place = place_ref[0]
    row = lax.broadcasted_iota(jnp.int32, (32, 128), 0)
    lane = lax.broadcasted_iota(jnp.int32, (32, 128), 1)
    prefix_len = lengths[0, 0]
    other_place = place + 1 - 2 * (place % 2)
    own = (row % 8 == place // 2) & ((lane < lengths[1, 0]) | (lane == 64))
    seen = (lane + place * 128 < prefix_len, lane + other_place * 128 < prefix_len, own)
    for i, mask in enumerate(seen):
        bias_ref[i] = jnp.where(mask, 0.0, MASKED)


def attend_kernel(
    place_ref,
    weight_hbm,
    query_ref,
    prefix_ref,
    other_ref,
    own_ref,
    bias_ref,
    out_ref,
    weight_ref,
    queries,
    arrived,
):
    copy = pltpu.make_async_copy(weight_hbm, weight_ref, arrived)
    copy.start()
    queries[...] = query_ref[...].reshape(CHIPS * HQ, 128).astype(F32)
    row = lax.broadcasted_iota(jnp.int32, (32, 128), 0)
    lane = lax.broadcasted_iota(jnp.int32, (32, 128), 1)
    mark = lane == row + 32 * (place_ref[0] // 2 % 4)
    ones = jnp.ones((384, 128), BF16)
    zeros = jnp.zeros((5, 128), F32)
    for k in range(KEY_VALUE_HEADS):
        head = slice(k * 128, (k + 1) * 128)
        parts = (prefix_ref, other_ref, own_ref)
        keys = jnp.concatenate([part[:128, head] for part in parts], axis=0)
        values = jnp.concatenate([part[128:, head] for part in parts], axis=0)
        query = [queries[pl.ds(k * GROUP + g, 8, stride=HQ), :] for g in range(GROUP)]
        query = jnp.concatenate(query, axis=0).astype(BF16)
        scores = lax.dot_general(
            query, keys, (((1,), (1,)), ((), ())), preferred_element_type=F32
        )
        scores = [scores[:, 128 * i : 128 * i + 128] * SCALE + bias_ref[i] for i in range(3)]
        top = jnp.maximum(jnp.maximum(scores[0], scores[1]), scores[2])
        top = jnp.max(top, axis=-1, keepdims=True)
        top = jnp.maximum(top, LOWEST).astype(BF16).astype(F32)
        weights = jnp.concatenate([jnp.exp(s - top) for s in scores], axis=1)
        summed = jnp.dot(
            weights.astype(BF16),
            jnp.concatenate([values, ones], axis=1),
            preferred_element_type=F32,
        )
        total = summed[:, 128:]
        total_high = total.astype(BF16).astype(F32)
        total_low = total - total_high
        out_ref[k, 0:32, :] = summed[:, :128].astype(BF16)
        stats = [
            jnp.sum(jnp.where(mark, v, 0.0), axis=0, keepdims=True)
            for v in (top, total_high, total_low)
        ]
        out_ref[k, 32:ROWS, :] = jnp.concatenate(stats + [zeros], axis=0).astype(BF16)
    copy.wait()


def project_kernel(place_ref, got_ref, own_ref, other_hbm, out_ref, rows, other_ref, arrived):
    copies = [
        pltpu.make_async_copy(
            other_hbm.at[:, n : n + WIDTH], other_ref.at[:, n : n + WIDTH], arrived.at[n // WIDTH]
        )
        for n in range(0, D, WIDTH)
    ]
    for copy in copies:
        copy.start()
    stats = got_ref[:, 32:ROWS, :].astype(F32)
    quads = [
        stats[4 * q] + stats[4 * q + 1] + stats[4 * q + 2] + stats[4 * q + 3] for q in range(2)
    ]
    tops = [s[0:1] for s in quads]
    totals = [s[1:2] + s[2:3] for s in quads]
    top = jnp.maximum(tops[0], tops[1])
    top = jnp.maximum(top, pltpu.roll(top, 64, 1))
    top = jnp.maximum(top, pltpu.roll(top, 32, 1))
    factors = [jnp.exp(t - top) for t in tops]
    total = sum(f * t for f, t in zip(factors, totals))
    total = total + pltpu.roll(total, 64, 1)
    total = total + pltpu.roll(total, 32, 1)
    row = lax.broadcasted_iota(jnp.int32, (32, 128), 0)
    lane = lax.broadcasted_iota(jnp.int32, (32, 128), 1)
    diagonal = lane % 32 == row
    mix = jnp.concatenate([jnp.where(diagonal, f / total, 0.0) for f in factors], axis=1)
    high = mix.astype(BF16)
    low = (mix - high.astype(F32)).astype(BF16)
    sums = got_ref[:, 0:32, :].reshape(CHIPS * 32, 128)
    both = jnp.dot(jnp.concatenate([high, low], axis=0), sums, preferred_element_type=F32)
    attn = both[:32] + both[32:]
    attn = jnp.concatenate([attn[8 * g : 8 * g + 8] for g in range(GROUP)], axis=1)
    north = place_ref[0] % 2 == 1
    mine = jnp.where(north, attn[:, 256:], attn[:, :256]).astype(BF16)
    others = jnp.where(north, attn[:, :256], attn[:, 256:]).astype(BF16)
    for n in range(0, D, WIDTH):
        cols = slice(n, n + WIDTH)
        piece = jnp.dot(mine, own_ref[:, cols], preferred_element_type=F32)
        copies[n // WIDTH].wait()
        piece += jnp.dot(others, other_ref[:, cols], preferred_element_type=F32)
        for i in range(WIDTH // 128):
            rows[pl.ds(n // 128 + i, 8, stride=BLOCKS), :] = piece[:, 128 * i : 128 * i + 128]
    out_ref[...] = rows[...].astype(BF16).reshape(CHIPS, BLOCKS, 128)


def finish_kernel(got_ref, residual_ref, gain_ref, hidden_ref, normed_ref):
    proj = got_ref[0].astype(F32)
    for i in range(1, CHIPS):
        proj += got_ref[i].astype(F32)
    stream = residual_ref[...] + proj
    scale = lax.rsqrt(jnp.sum(stream * stream) * (1.0 / D) + 1e-05)
    normed = stream * scale * gain_ref[...]
    for i in range(BLOCKS):
        cols = slice(128 * i, 128 * i + 128)
        hidden_ref[0:1, cols] = stream[i : i + 1].astype(BF16)
        normed_ref[0:1, cols] = normed[i : i + 1].astype(BF16)


def local(
    query_new,
    key_new,
    value_new,
    prefix_keys,
    prefix_values,
    sample_suffix_keys,
    sample_suffix_values,
    prefix_len,
    suffix_len,
    residual,
    out_weight,
    norm_gain,
):
    place = lax.axis_index("mp").astype(jnp.int32)[None]
    cores = [[2 * z + c for z in range(CHIPS)] for c in range(2)]
    swapped = [(i, i ^ 1) for i in range(SAMPLES)]
    spread = pl.pallas_call(
        spread_kernel,
        out_shape=jax.ShapeDtypeStruct((CHIPS, HQ, 128), BF16),
        in_specs=vmem(1),
        out_specs=vmem(1)[0],
        compiler_params=at_most(2),
        cost_estimate=LONG,
    )(query_new)
    queries = lax.all_to_all(spread, "mp", 0, 0, tiled=True, axis_index_groups=cores)
    prefix, own, bias, residual_rows, gain_rows = pl.pallas_call(
        stage_kernel,
        out_shape=[
            jax.ShapeDtypeStruct((256, 1024), BF16),
            jax.ShapeDtypeStruct((256, 1024), BF16),
            jax.ShapeDtypeStruct((3, 32, 128), F32),
            jax.ShapeDtypeStruct((BLOCKS, 128), F32),
            jax.ShapeDtypeStruct((BLOCKS, 128), F32),
        ],
        in_specs=smem(1) + hbm(2) + vmem(8),
        out_specs=vmem(5),
        scratch_shapes=[pltpu.SMEM((2, 1), jnp.int32), pltpu.SemaphoreType.DMA((2,))],
        compiler_params=at_most(4),
        cost_estimate=LONG,
    )(
        place,
        prefix_len,
        suffix_len,
        prefix_keys,
        prefix_values,
        sample_suffix_keys,
        sample_suffix_values,
        key_new,
        value_new,
        residual,
        norm_gain.reshape(BLOCKS, 128),
    )
    other_prefix = lax.ppermute(prefix, "mp", swapped)
    other_weight = lax.ppermute(out_weight, "mp", swapped)
    partial, weight = pl.pallas_call(
        attend_kernel,
        out_shape=[
            jax.ShapeDtypeStruct((CHIPS, ROWS, 128), BF16),
            jax.ShapeDtypeStruct((256, D), BF16),
        ],
        in_specs=smem(1) + hbm(1) + vmem(5),
        out_specs=vmem(2),
        scratch_shapes=[pltpu.VMEM((CHIPS * HQ, 128), F32), pltpu.SemaphoreType.DMA],
        compiler_params=at_most(12),
        cost_estimate=LONG,
    )(place, out_weight, queries, prefix, other_prefix, own, bias)
    partial = lax.all_to_all(partial, "mp", 0, 0, tiled=True, axis_index_groups=cores)
    proj = pl.pallas_call(
        project_kernel,
        out_shape=jax.ShapeDtypeStruct((CHIPS, BLOCKS, 128), BF16),
        in_specs=smem(1) + vmem(2) + hbm(1),
        out_specs=vmem(1)[0],
        scratch_shapes=[
            pltpu.VMEM((8 * BLOCKS, 128), F32),
            pltpu.VMEM((256, D), BF16),
            pltpu.SemaphoreType.DMA((D // WIDTH,)),
        ],
        compiler_params=at_most(16),
        cost_estimate=LONG,
    )(place, partial, weight, other_weight)
    proj = lax.all_to_all(proj, "mp", 0, 0, tiled=True, axis_index_groups=cores)
    return tuple(
        pl.pallas_call(
            finish_kernel,
            out_shape=[jax.ShapeDtypeStruct((1, D), BF16)] * 2,
            in_specs=vmem(3),
            out_specs=vmem(2),
            compiler_params=at_most(4),
        )(proj, residual_rows, gain_rows)
    )


def solution(mesh):
    whole = P(("dp", "mp"), None)
    placed = (
        whole,
        whole,
        whole,
        whole,
        whole,
        P(("dp", "mp"), None, None),
        P(("dp", "mp"), None, None),
        P("dp"),
        P(("dp", "mp")),
        whole,
        P("mp", None),
        P(),
    )

    def step(*arrays):
        return local(*arrays)

    step = jax.shard_map(
        step, mesh=mesh, in_specs=placed, out_specs=(whole, whole), check_vma=False
    )
    return step
```

time: 57.8 us -> 62.1 us (1.074)
  the two profiles are of different devices: /device:TPU:1 before, /device:TPU:6 now
where the time goes in v1:
time: 62.1 us; the launch traced here: 61.5 us
  blocking collectives  40.9 us (66%)
  Pallas kernels  7.47 us (12%)
  local copies, waits for them, and re-layouts  6.56 us (11%)
  starting transfers between devices  4.59 us (7%)
  between operations  2.01 us (3%)
    all_to_all x1, blocking collectives, local(): lax.all_to_all(spread, 'mp', 0, 0, tiled=True, axis_index_groups=cores)  18.5 us
    all_to_all x1, blocking collectives, local(): proj = lax.all_to_all(proj, 'mp', 0, 0, tiled=True, axis_index_groups=cores)  11.5 us
    all_to_all x1, blocking collectives, local(): lax.all_to_all(partial, 'mp', 0, 0, tiled=True, axis_index_groups=cores)  10.9 us
    unnamed x20, local copies, waits for them, and re-layouts  6.56 us
    pallas_call x1, Pallas kernels, local(): pl.pallas_call(project_kernel, out_shape=jax.ShapeDtypeStruct((CHIPS, BLO...  3.5 us
    ppermute x1, starting transfers between devices, local(): other_prefix = lax.ppermute(prefix, 'mp', swapped)  2.67 us
    pallas_call x1, Pallas kernels, local(): pl.pallas_call(attend_kernel, out_shape=[jax.ShapeDtypeStruct((CHIPS, ROW...  2.55 us
    ppermute x1, starting transfers between devices, local(): other_weight = lax.ppermute(out_weight, 'mp', swapped)  1.92 us
  transfers between devices with their start and end apart: 2, of which 0 were waited for; matrix products, arithmetic and copies ran while one was open for 0% of the time, Pallas kernels for 5%

profile of v1, /device:TPU:6, one launch (start us, length us, event | category | flops | bytes accessed | tf_op | source)
XLA Modules:
  0.0 61.5 jit_solution(14645239278924753608)
XLA Ops:
  0.6 1.9 %collective-permute-start.1 = (bf16[256,8192]{1,0:T(8,128)(2,1)}, bf16[256,8192]{1,0:T(8,128)(2,1)}, u32[]{:S(2)}, u32[]{:S(2)}) collective-permute-start(bf16[256,8192]{1,0:T(8,128)(2,1)} %weight_hbm.1), channel_id=1, source_target_pairs={{0,1},{1,0},{2,3},{3,2},{4,5},{5,4},{6,7},{7,6},{8,9},{9,8},{10,11... | collective-permute-start | bytes 12582920 | tf_op jit(solution)/shard_map/ppermute | solution.py:265
  3.9 0.0 copy-start.1
  3.9 0.9 %copy-done.1 = bf16[128,1024]{1,0:T(8,128)(2,1)S(1)} copy-done((bf16[128,1024]{1,0:T(8,128)(2,1)S(1)}, bf16[128,1024]{1,0:T(8,128)(2,1)}, u32[]{:S(2)}) %copy-start.1) | copy-done | bytes 262168
  4.8 0.0 copy-start.2
  4.8 0.9 %copy-done.2 = bf16[128,1024]{1,0:T(8,128)(2,1)S(1)} copy-done((bf16[128,1024]{1,0:T(8,128)(2,1)S(1)}, bf16[128,1024]{1,0:T(8,128)(2,1)}, u32[]{:S(2)}) %copy-start.2) | copy-done | bytes 262168
  5.8 0.0 copy-start.3
  5.8 0.9 %copy-done.3 = bf16[1,64,1024]{2,1,0:T(8,128)(2,1)S(1)} copy-done((bf16[1,64,1024]{2,1,0:T(8,128)(2,1)S(1)}, bf16[1,64,1024]{2,1,0:T(8,128)(2,1)}, u32[]{:S(2)}) %copy-start.3) | copy-done | bytes 131096
  6.7 0.0 copy-start.4
  6.7 0.9 %copy-done.4 = bf16[1,64,1024]{2,1,0:T(8,128)(2,1)S(1)} copy-done((bf16[1,64,1024]{2,1,0:T(8,128)(2,1)S(1)}, bf16[1,64,1024]{2,1,0:T(8,128)(2,1)}, u32[]{:S(2)}) %copy-start.4) | copy-done | bytes 131096
  7.6 0.0 copy-start.5
  7.6 0.8 %copy-done.5 = bf16[1,8192]{1,0:T(2,128)(2,1)S(1)} copy-done((bf16[1,8192]{1,0:T(2,128)(2,1)S(1)}, bf16[1,8192]{1,0:T(2,128)(2,1)}, u32[]{:S(2)}) %copy-start.5) | copy-done | bytes 16408
  8.3 0.0 copy-start.6
  8.3 0.7 %copy-done.6 = bf16[8192]{0:T(1024)(128)(2,1)S(1)} copy-done((bf16[8192]{0:T(1024)(128)(2,1)S(1)}, bf16[8192]{0:T(1024)(128)(2,1)}, u32[]{:S(2)}) %copy-start.6) | copy-done | bytes 16408
  9.0 0.0 copy-start.8
  9.0 0.7 %copy-done.8 = bf16[1,1024]{1,0:T(2,128)(2,1)S(1)} copy-done((bf16[1,1024]{1,0:T(2,128)(2,1)S(1)}, bf16[1,1024]{1,0:T(2,128)(2,1)}, u32[]{:S(2)}) %copy-start.8) | copy-done | bytes 2072
  9.7 0.0 copy-start.9
  9.7 0.7 %copy-done.9 = bf16[1,1024]{1,0:T(2,128)(2,1)S(1)} copy-done((bf16[1,1024]{1,0:T(2,128)(2,1)S(1)}, bf16[1,1024]{1,0:T(2,128)(2,1)}, u32[]{:S(2)}) %copy-start.9) | copy-done | bytes 2072
  10.4 0.0 copy-start.7
  10.4 0.6 shard_map.132
  11.0 0.0 copy-start
  11.0 2.7 %collective-permute-start = (bf16[256,1024]{1,0:T(8,128)(2,1)S(1)}, bf16[256,1024]{1,0:T(8,128)(2,1)S(1)}, u32[]{:S(2)}, u32[]{:S(2)}) collective-permute-start(bf16[256,1024]{1,0:T(8,128)(2,1)S(1)} %get-tuple-element.9.prefix_ref), channel_id=1, source_target_pairs={{0,1},{1,0},{2,3},{3,2},{4,5},{5,4},{6,7},{7,6},{8,9},{9,8},{10,11... | collective-permute-start | bytes 1572872 | tf_op jit(solution)/shard_map/ppermute | solution.py:264
  13.7 0.0 copy-done.7
  13.7 18.5 %all_to_all.15.query_ref = bf16[8,32,128]{2,1,0:T(8,128)(2,1)S(1)} all-to-all(bf16[8,32,128]{2,1,0:T(8,128)(2,1)S(1)} %shard_map.131), channel_id=1, replica_groups={{0,2,4,6,8,10,12,14},{1,3,5,7,9,11,13,15},{16,18,20,22,24,26,28,30},{17..., dimensions={0} | all-to-all | bytes 131072 | tf_op jit(solution)/shard_map/all_to_all | solution.py:236
  32.2 0.0 collective-permute-done.other_ref
  32.2 0.0 copy-done
  32.2 2.5 %shard_map.133 = (bf16[8,40,128]{2,1,0:T(8,128)(2,1)S(1)}, bf16[256,8192]{1,0:T(8,128)(2,1)S(1)}) custom-call(s32[1]{0:T(128)} %bitcast.place_ref, bf16[256,8192]{1,0:T(8,128)(2,1)S(1)} %copy-done, bf16[8,32,128]{2,1,0:T(8,128)(2,1)S(1)} %all_to_all.15.query_ref, bf16[256,1024]{1,0:T(8,128)(2,1)S(1)} %get-tuple-element.9.prefix_ref, ...), custom_call_target="tpu_custom_call" | custom-call | flops 10000000000 | bytes 1000000 | tf_op jit(solution)/shard_map/pallas_call | solution.py:266
  34.8 10.9 %all_to_all.16.got_ref = bf16[8,40,128]{2,1,0:T(8,128)(2,1)S(1)} all-to-all(bf16[8,40,128]{2,1,0:T(8,128)(2,1)S(1)} %get-tuple-element.12), channel_id=1, replica_groups={{0,2,4,6,8,10,12,14},{1,3,5,7,9,11,13,15},{16,18,20,22,24,26,28,30},{17..., dimensions={0} | all-to-all | bytes 163840 | tf_op jit(solution)/shard_map/all_to_all | solution.py:278
  45.7 0.0 collective-permute-done.1.other_hbm
  45.7 3.5 %shard_map.134 = bf16[8,64,128]{2,1,0:T(8,128)(2,1)S(1)} custom-call(s32[1]{0:T(128)} %bitcast.place_ref, bf16[8,40,128]{2,1,0:T(8,128)(2,1)S(1)} %all_to_all.16.got_ref, bf16[256,8192]{1,0:T(8,128)(2,1)S(1)} %get-tuple-element.13.own_ref, bf16[256,8192]{1,0:T(8,128)(2,1)} %collective-permute-done.1.other_hbm), custom_call_target="tpu_custom_call" | custom-call | flops 10000000000 | bytes 1000000 | tf_op jit(solution)/shard_map/pallas_call | solution.py:279
  49.2 11.5 %all_to_all.17.got_ref = bf16[8,64,128]{2,1,0:T(8,128)(2,1)S(1)} all-to-all(bf16[8,64,128]{2,1,0:T(8,128)(2,1)S(1)} %shard_map.134), channel_id=1, replica_groups={{0,2,4,6,8,10,12,14},{1,3,5,7,9,11,13,15},{16,18,20,22,24,26,28,30},{17..., dimensions={0} | all-to-all | bytes 262144 | tf_op jit(solution)/shard_map/all_to_all | solution.py:292
  60.7 0.8 %shard_map.135 = (bf16[1,8192]{1,0:T(2,128)(2,1)}, bf16[1,8192]{1,0:T(2,128)(2,1)}) custom-call(bf16[8,64,128]{2,1,0:T(8,128)(2,1)S(1)} %all_to_all.17.got_ref, f32[64,128]{1,0:T(8,128)S(1)} %get-tuple-element.14.residual_ref, f32[64,128]{1,0:T(8,128)S(1)} %get-tuple-element.15.gain_ref), custom_call_target="tpu_custom_call" | custom-call | tf_op jit(solution)/shard_map/pallas_call | solution.py:294
  (1 shorter events, 0.0 us)
Async XLA Ops:
  0.6 45.1 %collective-permute-start.1 = (bf16[256,8192]{1,0:T(8,128)(2,1)}, bf16[256,8192]{1,0:T(8,128)(2,1)}, u32[]{:S(2)}, u32[]{:S(2)}) collective-permute-start(bf16[256,8192]{1,0:T(8,128)(2,1)} %weight_hbm.1), channel_id=1, source_target_pairs={{0,1},{1,0},{2,3},{3,2},{4,5},{5,4},{6,7},{7,6},{8,9},{9,8},{10,11... | collective-permute-start | bytes 12582920 | tf_op jit(solution)/shard_map/ppermute | solution.py:265
  3.9 1.0 %copy-start.1 = (bf16[128,1024]{1,0:T(8,128)(2,1)S(1)}, bf16[128,1024]{1,0:T(8,128)(2,1)}, u32[]{:S(2)}) copy-start(bf16[128,1024]{1,0:T(8,128)(2,1)} %pkeys_ref.1) | copy-start | bytes 786436
  4.8 0.9 %copy-start.2 = (bf16[128,1024]{1,0:T(8,128)(2,1)S(1)}, bf16[128,1024]{1,0:T(8,128)(2,1)}, u32[]{:S(2)}) copy-start(bf16[128,1024]{1,0:T(8,128)(2,1)} %pvalues_ref.1) | copy-start | bytes 786436
  5.8 0.9 %copy-start.3 = (bf16[1,64,1024]{2,1,0:T(8,128)(2,1)S(1)}, bf16[1,64,1024]{2,1,0:T(8,128)(2,1)}, u32[]{:S(2)}) copy-start(bf16[1,64,1024]{2,1,0:T(8,128)(2,1)} %skeys_ref.1) | copy-start | bytes 393220
  6.7 0.9 %copy-start.4 = (bf16[1,64,1024]{2,1,0:T(8,128)(2,1)S(1)}, bf16[1,64,1024]{2,1,0:T(8,128)(2,1)}, u32[]{:S(2)}) copy-start(bf16[1,64,1024]{2,1,0:T(8,128)(2,1)} %svalues_ref.1) | copy-start | bytes 393220
  7.6 0.8 %copy-start.5 = (bf16[1,8192]{1,0:T(2,128)(2,1)S(1)}, bf16[1,8192]{1,0:T(2,128)(2,1)}, u32[]{:S(2)}) copy-start(bf16[1,8192]{1,0:T(2,128)(2,1)} %residual_ref.1) | copy-start | bytes 49156
  8.3 0.7 %copy-start.6 = (bf16[8192]{0:T(1024)(128)(2,1)S(1)}, bf16[8192]{0:T(1024)(128)(2,1)}, u32[]{:S(2)}) copy-start(bf16[8192]{0:T(1024)(128)(2,1)} %param.23) | copy-start | bytes 49156
  9.0 0.7 %copy-start.8 = (bf16[1,1024]{1,0:T(2,128)(2,1)S(1)}, bf16[1,1024]{1,0:T(2,128)(2,1)}, u32[]{:S(2)}) copy-start(bf16[1,1024]{1,0:T(2,128)(2,1)} %key_ref.1) | copy-start | bytes 6148
  9.7 0.7 %copy-start.9 = (bf16[1,1024]{1,0:T(2,128)(2,1)S(1)}, bf16[1,1024]{1,0:T(2,128)(2,1)}, u32[]{:S(2)}) copy-start(bf16[1,1024]{1,0:T(2,128)(2,1)} %value_ref.1) | copy-start | bytes 6148
  10.4 3.3 %copy-start.7 = (bf16[1,4096]{1,0:T(2,128)(2,1)S(1)}, bf16[1,4096]{1,0:T(2,128)(2,1)}, u32[]{:S(2)}) copy-start(bf16[1,4096]{1,0:T(2,128)(2,1)} %query_ref.1) | copy-start | bytes 24580
  11.0 21.2 %copy-start = (bf16[256,8192]{1,0:T(8,128)(2,1)S(1)}, bf16[256,8192]{1,0:T(8,128)(2,1)}, u32[]{:S(2)}) copy-start(bf16[256,8192]{1,0:T(8,128)(2,1)} %weight_hbm.1) | copy-start | bytes 12582916
  11.0 21.2 %collective-permute-start = (bf16[256,1024]{1,0:T(8,128)(2,1)S(1)}, bf16[256,1024]{1,0:T(8,128)(2,1)S(1)}, u32[]{:S(2)}, u32[]{:S(2)}) collective-permute-start(bf16[256,1024]{1,0:T(8,128)(2,1)S(1)} %get-tuple-element.9.prefix_ref), channel_id=1, source_target_pairs={{0,1},{1,0},{2,3},{3,2},{4,5},{5,4},{6,7},{7,6},{8,9},{9,8},{10,11... | collective-permute-start | bytes 1572872 | tf_op jit(solution)/shard_map/ppermute | solution.py:264

commit v2 on v0

--- a/solution.py
+++ b/solution.py
@@ -29,6 +29,10 @@
     return [pl.BlockSpec(memory_space=pltpu.VMEM)] * count
 
 
+def hbm(count):
+    return [pl.BlockSpec(memory_space=pltpu.HBM)] * count
+
+
 def at_most(mebibytes):
     return pltpu.CompilerParams(vmem_limit_bytes=mebibytes * 2**20)
 
@@ -44,37 +48,51 @@
         out_ref[i] = rows
 
 
-def attend_kernel(
+def stage_kernel(
     place_ref,
     prefix_len_ref,
     suffix_len_ref,
-    query_ref,
-    pkeys_ref,
-    pvalues_ref,
     skeys_ref,
     svalues_ref,
     key_ref,
     value_ref,
-    out_ref,
-    queries,
+    residual_ref,
+    gain_ref,
+    own_ref,
+    bias_ref,
+    residual_rows_ref,
+    gain_rows_ref,
 ):
+    first = lax.broadcasted_iota(jnp.int32, (64, 1024), 0) == 0
+    own_ref[0:64] = skeys_ref[0]
+    own_ref[64:128] = jnp.where(first, key_ref[...].astype(F32), 0.0).astype(BF16)
+    own_ref[128:192] = svalues_ref[0]
+    own_ref[192:256] = jnp.where(first, value_ref[...].astype(F32), 0.0).astype(BF16)
+    rows = [residual_ref[0:1, 128 * i : 128 * i + 128].astype(F32) for i in range(BLOCKS)]
+    residual_rows_ref[...] = jnp.concatenate(rows, axis=0)
+    gain_rows_ref[...] = gain_ref[...].astype(F32)
     place = place_ref[0]
-    queries[...] = query_ref[...].reshape(SAMPLES * HQ, 128).astype(F32)
     row = lax.broadcasted_iota(jnp.int32, (64, 128), 0)
     lane = lax.broadcasted_iota(jnp.int32, (64, 128), 1)
     sample = 2 * (row % 8) + row // 32
-    prefix_seen = lane + place * 128 < prefix_len_ref[0]
-    own_seen = (sample == place) & ((lane < suffix_len_ref[0]) | (lane == 64))
-    first = row == 0
-    mark = lane[:32] == row[:32] + 32 * (place % 4)
+    own = (sample == place) & ((lane < suffix_len_ref[0]) | (lane == 64))
+    bias_ref[0] = jnp.where(lane + place * 128 < prefix_len_ref[0], 0.0, MASKED)
+    bias_ref[1] = jnp.where(own, 0.0, MASKED)
+
+
+def attend_kernel(
+    place_ref, query_ref, pkeys_ref, pvalues_ref, own_ref, bias_ref, out_ref, queries
+):
+    queries[...] = query_ref[...].reshape(SAMPLES * HQ, 128).astype(F32)
+    row = lax.broadcasted_iota(jnp.int32, (32, 128), 0)
+    lane = lax.broadcasted_iota(jnp.int32, (32, 128), 1)
+    mark = lane == row + 32 * (place_ref[0] % 4)
     ones = jnp.ones((256, 128), BF16)
     zeros = jnp.zeros((5, 128), F32)
     for k in range(KEY_VALUE_HEADS):
         head = slice(k * 128, (k + 1) * 128)
-        new_key = jnp.where(first, key_ref[0:1, head].astype(F32), 0.0).astype(BF16)
-        new_value = jnp.where(first, value_ref[0:1, head].astype(F32), 0.0).astype(BF16)
-        keys = jnp.concatenate([pkeys_ref[:, head], skeys_ref[0, :, head], new_key], axis=0)
-        values = jnp.concatenate([pvalues_ref[:, head], svalues_ref[0, :, head], new_value], axis=0)
+        keys = jnp.concatenate([pkeys_ref[:, head], own_ref[:128, head]], axis=0)
+        values = jnp.concatenate([pvalues_ref[:, head], own_ref[128:, head]], axis=0)
         query = [
             queries[pl.ds(c * HQ + k * GROUP + g, 8, stride=2 * HQ), :]
             for c in range(2)
@@ -84,8 +102,8 @@
         scores = lax.dot_general(
             query, keys, (((1,), (1,)), ((), ())), preferred_element_type=F32
         )
-        s_pre = jnp.where(prefix_seen, scores[:, :128] * SCALE, MASKED)
-        s_own = jnp.where(own_seen, scores[:, 128:] * SCALE, MASKED)
+        s_pre = scores[:, :128] * SCALE + bias_ref[0]
+        s_own = scores[:, 128:] * SCALE + bias_ref[1]
         top = jnp.max(jnp.maximum(s_pre, s_own), axis=-1, keepdims=True)
         top = jnp.maximum(top, LOWEST).astype(BF16).astype(F32)
         weights = jnp.concatenate([jnp.exp(s_pre - top), jnp.exp(s_own - top)], axis=1)
@@ -107,7 +125,7 @@
             out_ref[2 * k + c, 32:ROWS, :] = jnp.concatenate(stats + [zeros], axis=0).astype(BF16)
 
 
-def project_kernel(place_ref, got_ref, own_ref, other_hbm, out_ref, rows, other_ref, arrived):
+def project_kernel(place_ref, got_ref, own_ref, other_hbm, out_ref, halves, rows, other_ref, arrived):
     copies = [
         pltpu.make_async_copy(
             other_hbm.at[:, n : n + WIDTH], other_ref.at[:, n : n + WIDTH], arrived.at[n // WIDTH]
@@ -144,18 +162,14 @@
     others = jnp.where(north, attn[:, :256], attn[:, 256:]).astype(BF16)
     for n in range(0, D, WIDTH):
         cols = slice(n, n + WIDTH)
-        piece = jnp.dot(mine, own_ref[:, cols], preferred_element_type=F32)
-        copies[n // WIDTH].wait()
-        piece += jnp.dot(others, other_ref[:, cols], preferred_element_type=F32)
+        halves[:, cols] = jnp.dot(mine, own_ref[:, cols], preferred_element_type=F32)
+    for n, copy in zip(range(0, D, WIDTH), copies):
+        cols = slice(n, n + WIDTH)
+        copy.wait()
+        piece = halves[:, cols] + jnp.dot(others, other_ref[:, cols], preferred_element_type=F32)
         for i in range(WIDTH // 128):
             rows[pl.ds(n // 128 + i, 8, stride=BLOCKS), :] = piece[:, 128 * i : 128 * i + 128]
     out_ref[...] = rows[...].astype(BF16).reshape(CHIPS, BLOCKS, 128)
-
-
-def stage_kernel(residual_ref, gain_ref, residual_rows_ref, gain_rows_ref):
-    rows = [residual_ref[0:1, 128 * i : 128 * i + 128].astype(F32) for i in range(BLOCKS)]
-    residual_rows_ref[...] = jnp.concatenate(rows, axis=0)
-    gain_rows_ref[...] = gain_ref[...].astype(F32)
 
 
 def finish_kernel(got_ref, residual_ref, gain_ref, hidden_ref, normed_ref):
@@ -187,7 +201,6 @@
 ):
     place = lax.axis_index("mp").astype(jnp.int32)[None]
     cores = [[2 * z + c for z in range(CHIPS)] for c in range(2)]
-    other_weight = lax.ppermute(out_weight, "mp", [(i, i ^ 1) for i in range(SAMPLES)])
     spread = pl.pallas_call(
         spread_kernel,
         out_shape=jax.ShapeDtypeStruct((SAMPLES, HQ, 128), BF16),
@@ -197,41 +210,47 @@
         cost_estimate=LONG,
     )(query_new)
     queries = lax.all_to_all(spread, "mp", 0, 0, tiled=True)
-    residual_rows, gain_rows = pl.pallas_call(
+    own, bias, residual_rows, gain_rows = pl.pallas_call(
         stage_kernel,
-        out_shape=[jax.ShapeDtypeStruct((BLOCKS, 128), F32)] * 2,
-        in_specs=vmem(2),
-        out_specs=vmem(2),
-        compiler_params=at_most(2),
-        cost_estimate=LONG,
-    )(residual, norm_gain.reshape(BLOCKS, 128))
-    partial = pl.pallas_call(
-        attend_kernel,
-        out_shape=jax.ShapeDtypeStruct((SAMPLES, ROWS, 128), BF16),
-        in_specs=smem(3) + vmem(7),
-        out_specs=vmem(1)[0],
-        scratch_shapes=[pltpu.VMEM((SAMPLES * HQ, 128), F32)],
-        compiler_params=at_most(8),
+        out_shape=[
+            jax.ShapeDtypeStruct((256, 1024), BF16),
+            jax.ShapeDtypeStruct((2, 64, 128), F32),
+            jax.ShapeDtypeStruct((BLOCKS, 128), F32),
+            jax.ShapeDtypeStruct((BLOCKS, 128), F32),
+        ],
+        in_specs=smem(3) + vmem(6),
+        out_specs=vmem(4),
+        compiler_params=at_most(4),
         cost_estimate=LONG,
     )(
         place,
         prefix_len,
         suffix_len,
-        queries,
-        prefix_keys,
-        prefix_values,
         sample_suffix_keys,
         sample_suffix_values,
         key_new,
         value_new,
-    )
+        residual,
+        norm_gain.reshape(BLOCKS, 128),
+    )
+    other_weight = lax.ppermute(out_weight, "mp", [(i, i ^ 1) for i in range(SAMPLES)])
+    partial = pl.pallas_call(
+        attend_kernel,
+        out_shape=jax.ShapeDtypeStruct((SAMPLES, ROWS, 128), BF16),
+        in_specs=smem(1) + vmem(5),
+        out_specs=vmem(1)[0],
+        scratch_shapes=[pltpu.VMEM((SAMPLES * HQ, 128), F32)],
+        compiler_params=at_most(8),
+        cost_estimate=LONG,
+    )(place, queries, prefix_keys, prefix_values, own, bias)
     partial = lax.all_to_all(partial, "mp", 0, 0, tiled=True)
     proj = pl.pallas_call(
         project_kernel,
         out_shape=jax.ShapeDtypeStruct((CHIPS, BLOCKS, 128), BF16),
-        in_specs=smem(1) + vmem(2) + [pl.BlockSpec(memory_space=pl.ANY)],
+        in_specs=smem(1) + vmem(2) + hbm(1),
         out_specs=vmem(1)[0],
         scratch_shapes=[
+            pltpu.VMEM((8, D), F32),
             pltpu.VMEM((8 * BLOCKS, 128), F32),
             pltpu.VMEM((256, D), BF16),
             pltpu.SemaphoreType.DMA((D // WIDTH,)),

time: 57.8 us -> 52.9 us (0.915)
  blocking collectives: 12.2 us -> 23.1 us
  waiting for transfers between devices: 17.1 us -> 7.43 us
  starting transfers between devices: 17.4 us -> 14 us
  Pallas kernels: 7.94 us -> 5.1 us
    all_to_all x0 -> x1, blocking collectives: none -> 10.8 us  [local(): proj = lax.all_to_all(proj, 'mp', 0, 0, tiled=True, axis_index_groups=cores)]
    all_to_all x1 -> x0, waiting for transfers between devices: 9.46 us -> none  [local(): proj = lax.all_to_all(proj, 'mp', 0, 0, tiled=True, axis_index_groups=cores)]
    all_to_all x1 -> x0, starting transfers between devices: 3.38 us -> none  [local(): proj = lax.all_to_all(proj, 'mp', 0, 0, tiled=True, axis_index_groups=cores)]
    pallas_call x1, Pallas kernels: 2.26 us -> 0.71 us  [local(): pl.pallas_call(attend_kernel, out_shape=jax.ShapeDtypeStruct((SAMPLES, RO...]
    pallas_call x1, Pallas kernels: 4.15 us -> 2.83 us  [local(): pl.pallas_call(project_kernel, out_shape=jax.ShapeDtypeStruct((CHIPS, BLO...]
  transfers between devices with their start and end apart: 3 -> 2, of which waited for: 2 -> 1; matrix products, arithmetic and copies ran while one was open for 0% -> 0% of each run, Pallas kernels for 5% -> 3%
where the time goes in v2:
time: 52.9 us; the launch traced here: 52.4 us
  blocking collectives  23.1 us (44%)
  starting transfers between devices  14 us (26%)
  waiting for transfers between devices  7.43 us (14%)
  Pallas kernels  5.1 us (10%)
  between operations  2.06 us (4%)
  local copies, waits for them, and re-layouts  0.75 us (1%)
    all_to_all x1, blocking collectives, local(): partial = lax.all_to_all(partial, 'mp', 0, 0, tiled=True)  12.3 us
    all_to_all x1, blocking collectives, local(): proj = lax.all_to_all(proj, 'mp', 0, 0, tiled=True, axis_index_groups=cores)  10.8 us
    ppermute x1, starting transfers between devices, local(): lax.ppermute(out_weight, 'mp', [(i, i ^ 1) for i in range(SAMPLES)])  8.88 us
    all_to_all x1, waiting for transfers between devices, local(): queries = lax.all_to_all(spread, 'mp', 0, 0, tiled=True)  7.43 us
    all_to_all x1, starting transfers between devices, local(): queries = lax.all_to_all(spread, 'mp', 0, 0, tiled=True)  5.1 us
    pallas_call x1, Pallas kernels, local(): pl.pallas_call(project_kernel, out_shape=jax.ShapeDtypeStruct((CHIPS, BLO...  2.83 us
  transfers between devices with their start and end apart: 2, of which 1 were waited for; matrix products, arithmetic and copies ran while one was open for 0% of the time, Pallas kernels for 3%

profile of v2, /device:TPU:1, one launch (start us, length us, event | category | flops | bytes accessed | tf_op | source)
XLA Modules:
  0.0 52.4 jit_solution(8186991938409512552)
XLA Ops:
  0.6 0.0 copy-start.5
  0.6 0.0 copy-start.4
  0.7 0.0 copy-start.3
  0.7 8.9 %collective-permute-start = (bf16[256,8192]{1,0:T(8,128)(2,1)}, bf16[256,8192]{1,0:T(8,128)(2,1)}, u32[]{:S(2)}, u32[]{:S(2)}) collective-permute-start(bf16[256,8192]{1,0:T(8,128)(2,1)} %own_ref.1), channel_id=1, source_target_pairs={{0,1},{1,0},{2,3},{3,2},{4,5},{5,4},{6,7},{7,6},{8,9},{9,8},{10,11... | collective-permute-start | bytes 12582920 | tf_op jit(solution)/shard_map/ppermute | solution.py:236
  9.6 0.0 copy-start.6
  9.6 0.7 %copy-done.6 = bf16[1,4096]{1,0:T(2,128)(2,1)S(1)} copy-done((bf16[1,4096]{1,0:T(2,128)(2,1)S(1)}, bf16[1,4096]{1,0:T(2,128)(2,1)}, u32[]{:S(2)}) %copy-start.6) | copy-done | bytes 8216
  10.3 0.0 copy-start.7
  10.3 0.0 copy-start.8
  10.3 0.0 copy-start.9
  10.3 0.7 %shard_map.131 = bf16[16,32,128]{2,1,0:T(8,128)(2,1)} custom-call(bf16[1,4096]{1,0:T(2,128)(2,1)S(1)} %copy-done.6), custom_call_target="tpu_custom_call" | custom-call | flops 10000000000 | bytes 1000000 | tf_op jit(solution)/shard_map/pallas_call | solution.py:204
  10.9 5.1 %all-to-all-start = ((bf16[16,32,128]{2,1,0:T(8,128)(2,1)}), bf16[16,32,128]{2,1,0:T(8,128)(2,1)S(1)}, u32[]{:S(2)}, u32[]{:S(2)}) async-start(bf16[16,32,128]{2,1,0:T(8,128)(2,1)} %shard_map.131), calls=%async_computation | async-start | bytes 262144 | tf_op jit(solution)/shard_map/all_to_all | solution.py:212
  17.3 0.0 copy-done.5
  17.3 0.0 copy-done.4
  17.4 0.0 copy-done.3
  17.4 0.0 copy-done.7
  17.4 0.0 copy-done.8
  17.4 0.0 copy-done.9
  17.4 0.0 copy-start.1
  17.4 0.0 copy-start.2
  17.4 0.1 shard_map.132
  17.5 7.4 %all-to-all-done.query_ref = bf16[16,32,128]{2,1,0:T(8,128)(2,1)S(1)} async-done(((bf16[16,32,128]{2,1,0:T(8,128)(2,1)}), bf16[16,32,128]{2,1,0:T(8,128)(2,1)S(1)}, u32[]{:S(2)}, u32[]{:S(2)}) %all-to-all-start) | async-done | bytes 131104 | tf_op jit(solution)/shard_map/all_to_all | solution.py:212
  24.9 0.0 copy-done.1
  24.9 0.0 copy-done.2
  24.9 0.0 copy-start
  24.9 0.7 %shard_map.133 = bf16[16,40,128]{2,1,0:T(8,128)(2,1)S(1)} custom-call(s32[1]{0:T(128)} %bitcast.place_ref, bf16[16,32,128]{2,1,0:T(8,128)(2,1)S(1)} %all-to-all-done.query_ref, bf16[128,1024]{1,0:T(8,128)(2,1)S(1)} %copy-done.1, bf16[128,1024]{1,0:T(8,128)(2,1)S(1)} %copy-done.2, bf16[256,1024]{1,0:T(8,128)(2,1)S(1)} %get-tuple-element.6.own_ref, ...), custom_call_target="tpu_custom_call" | custom-call | flops 10000000000 | bytes 1000000 | tf_op jit(solution)/shard_map/pallas_call | solution.py:237
  25.6 12.3 %all_to_all.15.got_ref = bf16[16,40,128]{2,1,0:T(8,128)(2,1)S(1)} all-to-all(bf16[16,40,128]{2,1,0:T(8,128)(2,1)S(1)} %shard_map.133), channel_id=1, replica_groups=mesh['dp'=32,'mp'=16] {'mp'}, dimensions={0} | all-to-all | bytes 327680 | tf_op jit(solution)/shard_map/all_to_all | solution.py:246
  38.0 0.0 collective-permute-done.other_hbm
  38.0 0.0 copy-done
  38.0 2.8 %shard_map.134 = bf16[8,64,128]{2,1,0:T(8,128)(2,1)S(1)} custom-call(s32[1]{0:T(128)} %bitcast.place_ref, bf16[16,40,128]{2,1,0:T(8,128)(2,1)S(1)} %all_to_all.15.got_ref, bf16[256,8192]{1,0:T(8,128)(2,1)S(1)} %copy-done, bf16[256,8192]{1,0:T(8,128)(2,1)} %collective-permute-done.other_hbm), custom_call_target="tpu_custom_call" | custom-call | flops 10000000000 | bytes 1000000 | tf_op jit(solution)/shard_map/pallas_call | solution.py:247
  40.8 10.8 %all_to_all.16.got_ref = bf16[8,64,128]{2,1,0:T(8,128)(2,1)S(1)} all-to-all(bf16[8,64,128]{2,1,0:T(8,128)(2,1)S(1)} %shard_map.134), channel_id=1, replica_groups={{0,2,4,6,8,10,12,14},{1,3,5,7,9,11,13,15},{16,18,20,22,24,26,28,30},{17..., dimensions={0} | all-to-all | bytes 262144 | tf_op jit(solution)/shard_map/all_to_all | solution.py:261
  51.6 0.8 %shard_map.135 = (bf16[1,8192]{1,0:T(2,128)(2,1)}, bf16[1,8192]{1,0:T(2,128)(2,1)}) custom-call(bf16[8,64,128]{2,1,0:T(8,128)(2,1)S(1)} %all_to_all.16.got_ref, f32[64,128]{1,0:T(8,128)S(1)} %get-tuple-element.8.residual_ref, f32[64,128]{1,0:T(8,128)S(1)} %get-tuple-element.9.gain_ref), custom_call_target="tpu_custom_call" | custom-call | tf_op jit(solution)/shard_map/pallas_call | solution.py:263
Async XLA Ops:
  0.6 16.7 %copy-start.5 = (bf16[1,8192]{1,0:T(2,128)(2,1)S(1)}, bf16[1,8192]{1,0:T(2,128)(2,1)}, u32[]{:S(2)}) copy-start(bf16[1,8192]{1,0:T(2,128)(2,1)} %residual_ref.1) | copy-start | bytes 49156
  0.6 16.7 %copy-start.4 = (bf16[1,64,1024]{2,1,0:T(8,128)(2,1)S(1)}, bf16[1,64,1024]{2,1,0:T(8,128)(2,1)}, u32[]{:S(2)}) copy-start(bf16[1,64,1024]{2,1,0:T(8,128)(2,1)} %svalues_ref.1) | copy-start | bytes 393220
  0.7 16.7 %copy-start.3 = (bf16[1,64,1024]{2,1,0:T(8,128)(2,1)S(1)}, bf16[1,64,1024]{2,1,0:T(8,128)(2,1)}, u32[]{:S(2)}) copy-start(bf16[1,64,1024]{2,1,0:T(8,128)(2,1)} %skeys_ref.1) | copy-start | bytes 393220
  0.7 37.3 %collective-permute-start = (bf16[256,8192]{1,0:T(8,128)(2,1)}, bf16[256,8192]{1,0:T(8,128)(2,1)}, u32[]{:S(2)}, u32[]{:S(2)}) collective-permute-start(bf16[256,8192]{1,0:T(8,128)(2,1)} %own_ref.1), channel_id=1, source_target_pairs={{0,1},{1,0},{2,3},{3,2},{4,5},{5,4},{6,7},{7,6},{8,9},{9,8},{10,11... | collective-permute-start | bytes 12582920 | tf_op jit(solution)/shard_map/ppermute | solution.py:236
  9.6 0.7 %copy-start.6 = (bf16[1,4096]{1,0:T(2,128)(2,1)S(1)}, bf16[1,4096]{1,0:T(2,128)(2,1)}, u32[]{:S(2)}) copy-start(bf16[1,4096]{1,0:T(2,128)(2,1)} %query_ref.1) | copy-start | bytes 24580
  10.3 7.1 %copy-start.7 = (bf16[8192]{0:T(1024)(128)(2,1)S(1)}, bf16[8192]{0:T(1024)(128)(2,1)}, u32[]{:S(2)}) copy-start(bf16[8192]{0:T(1024)(128)(2,1)} %param.23) | copy-start | bytes 49156
  10.3 7.1 %copy-start.8 = (bf16[1,1024]{1,0:T(2,128)(2,1)S(1)}, bf16[1,1024]{1,0:T(2,128)(2,1)}, u32[]{:S(2)}) copy-start(bf16[1,1024]{1,0:T(2,128)(2,1)} %key_ref.1) | copy-start | bytes 6148
  10.3 7.1 %copy-start.9 = (bf16[1,1024]{1,0:T(2,128)(2,1)S(1)}, bf16[1,1024]{1,0:T(2,128)(2,1)}, u32[]{:S(2)}) copy-start(bf16[1,1024]{1,0:T(2,128)(2,1)} %value_ref.1) | copy-start | bytes 6148
  10.9 14.0 %all-to-all-start = ((bf16[16,32,128]{2,1,0:T(8,128)(2,1)}), bf16[16,32,128]{2,1,0:T(8,128)(2,1)S(1)}, u32[]{:S(2)}, u32[]{:S(2)}) async-start(bf16[16,32,128]{2,1,0:T(8,128)(2,1)} %shard_map.131), calls=%async_computation | async-start | bytes 262144 | tf_op jit(solution)/shard_map/all_to_all | solution.py:212
  17.4 7.5 %copy-start.1 = (bf16[128,1024]{1,0:T(8,128)(2,1)S(1)}, bf16[128,1024]{1,0:T(8,128)(2,1)}, u32[]{:S(2)}) copy-start(bf16[128,1024]{1,0:T(8,128)(2,1)} %pkeys_ref.1) | copy-start | bytes 786436
  17.4 7.5 %copy-start.2 = (bf16[128,1024]{1,0:T(8,128)(2,1)S(1)}, bf16[128,1024]{1,0:T(8,128)(2,1)}, u32[]{:S(2)}) copy-start(bf16[128,1024]{1,0:T(8,128)(2,1)} %pvalues_ref.1) | copy-start | bytes 786436
  24.9 13.1 %copy-start = (bf16[256,8192]{1,0:T(8,128)(2,1)S(1)}, bf16[256,8192]{1,0:T(8,128)(2,1)}, u32[]{:S(2)}) copy-start(bf16[256,8192]{1,0:T(8,128)(2,1)} %own_ref.1) | copy-start | bytes 12582916

commit v3 on v2

--- a/solution.py
+++ b/solution.py
@@ -14,8 +14,8 @@
 CHIPS = 8
 D = 8192
 BLOCKS = D // 128
-WIDTH = 1024
-ROWS = 40
+WIDTH = 2048
+ROWS = 18
 SCALE = HEAD_SIZE ** (-0.5)
 MASKED = -1e30
 LOWEST = -1e29
@@ -88,7 +88,7 @@
     lane = lax.broadcasted_iota(jnp.int32, (32, 128), 1)
     mark = lane == row + 32 * (place_ref[0] % 4)
     ones = jnp.ones((256, 128), BF16)
-    zeros = jnp.zeros((5, 128), F32)
+    zeros = jnp.zeros((1, 128), F32)
     for k in range(KEY_VALUE_HEADS):
         head = slice(k * 128, (k + 1) * 128)
         keys = jnp.concatenate([pkeys_ref[:, head], own_ref[:128, head]], axis=0)
@@ -117,12 +117,12 @@
         total_low = total - total_high
         for c in range(2):
             part = slice(32 * c, 32 * c + 32)
-            out_ref[2 * k + c, 0:32, :] = summed[part, :128].astype(BF16)
+            out_ref[2 * k + c, 0:16] = summed[part, :128].astype(BF16).reshape(16, 2, 128)
             stats = [
                 jnp.sum(jnp.where(mark, v[part], 0.0), axis=0, keepdims=True)
                 for v in (top, total_high, total_low)
             ]
-            out_ref[2 * k + c, 32:ROWS, :] = jnp.concatenate(stats + [zeros], axis=0).astype(BF16)
+            out_ref[2 * k + c, 16:ROWS] = jnp.concatenate(stats + [zeros], axis=0).astype(BF16).reshape(2, 2, 128)
 
 
 def project_kernel(place_ref, got_ref, own_ref, other_hbm, out_ref, halves, rows, other_ref, arrived):
@@ -134,7 +134,7 @@
     ]
     for copy in copies:
         copy.start()
-    stats = got_ref[:, 32:ROWS, :].astype(F32)
+    stats = got_ref[:, 16:ROWS].reshape(SAMPLES, 4, 128).astype(F32)
     quads = [
         stats[4 * q] + stats[4 * q + 1] + stats[4 * q + 2] + stats[4 * q + 3] for q in range(4)
     ]
@@ -153,7 +153,7 @@
     mix = jnp.concatenate([jnp.where(diagonal, f / total, 0.0) for f in factors], axis=1)
     high = mix.astype(BF16)
     low = (mix - high.astype(F32)).astype(BF16)
-    sums = got_ref[:, 0:32, :].reshape(SAMPLES * 32, 128)
+    sums = got_ref[:, 0:16].reshape(SAMPLES * 32, 128)
     both = jnp.dot(jnp.concatenate([high, low], axis=0), sums, preferred_element_type=F32)
     attn = both[:32] + both[32:]
     attn = jnp.concatenate([attn[8 * g : 8 * g + 8] for g in range(GROUP)], axis=1)
@@ -236,7 +236,7 @@
     other_weight = lax.ppermute(out_weight, "mp", [(i, i ^ 1) for i in range(SAMPLES)])
     partial = pl.pallas_call(
         attend_kernel,
-        out_shape=jax.ShapeDtypeStruct((SAMPLES, ROWS, 128), BF16),
+        out_shape=jax.ShapeDtypeStruct((SAMPLES, ROWS, 2, 128), BF16),
         in_specs=smem(1) + vmem(5),
         out_specs=vmem(1)[0],
         scratch_shapes=[pltpu.VMEM((SAMPLES * HQ, 128), F32)],

time: 52.9 us -> 52.4 us (level)
  no operation moved by 1% of the time
where the time goes in v3:
time: 52.4 us; the launch traced here: 51.9 us
  blocking collectives  22.9 us (44%)
  starting transfers between devices  14 us (27%)
  waiting for transfers between devices  7.43 us (14%)
  Pallas kernels  4.85 us (9%)
  between operations  2.06 us (4%)
  local copies, waits for them, and re-layouts  0.75 us (1%)
    all_to_all x1, blocking collectives, local(): partial = lax.all_to_all(partial, 'mp', 0, 0, tiled=True)  12 us
    all_to_all x1, blocking collectives, local(): proj = lax.all_to_all(proj, 'mp', 0, 0, tiled=True, axis_index_groups=cores)  10.8 us
    ppermute x1, starting transfers between devices, local(): lax.ppermute(out_weight, 'mp', [(i, i ^ 1) for i in range(SAMPLES)])  8.88 us
    all_to_all x1, waiting for transfers between devices, local(): queries = lax.all_to_all(spread, 'mp', 0, 0, tiled=True)  7.43 us
    all_to_all x1, starting transfers between devices, local(): queries = lax.all_to_all(spread, 'mp', 0, 0, tiled=True)  5.1 us
    pallas_call x1, Pallas kernels, local(): pl.pallas_call(project_kernel, out_shape=jax.ShapeDtypeStruct((CHIPS, BLO...  2.56 us
  transfers between devices with their start and end apart: 2, of which 1 were waited for; matrix products, arithmetic and copies ran while one was open for 0% of the time, Pallas kernels for 3%

profile of v3, /device:TPU:1, one launch (start us, length us, event | category | flops | bytes accessed | tf_op | source)
XLA Modules:
  0.0 51.9 jit_solution(14802730511271162256)
XLA Ops:
  0.6 0.0 copy-start.5
  0.6 0.0 copy-start.4
  0.7 0.0 copy-start.3
  0.7 8.9 %collective-permute-start = (bf16[256,8192]{1,0:T(8,128)(2,1)}, bf16[256,8192]{1,0:T(8,128)(2,1)}, u32[]{:S(2)}, u32[]{:S(2)}) collective-permute-start(bf16[256,8192]{1,0:T(8,128)(2,1)} %own_ref.1), channel_id=1, source_target_pairs={{0,1},{1,0},{2,3},{3,2},{4,5},{5,4},{6,7},{7,6},{8,9},{9,8},{10,11... | collective-permute-start | bytes 12582920 | tf_op jit(solution)/shard_map/ppermute | solution.py:236
  9.6 0.0 copy-start.6
  9.6 0.7 %copy-done.6 = bf16[1,4096]{1,0:T(2,128)(2,1)S(1)} copy-done((bf16[1,4096]{1,0:T(2,128)(2,1)S(1)}, bf16[1,4096]{1,0:T(2,128)(2,1)}, u32[]{:S(2)}) %copy-start.6) | copy-done | bytes 8216
  10.3 0.0 copy-start.7
  10.3 0.0 copy-start.8
  10.3 0.0 copy-start.9
  10.3 0.7 %shard_map.131 = bf16[16,32,128]{2,1,0:T(8,128)(2,1)} custom-call(bf16[1,4096]{1,0:T(2,128)(2,1)S(1)} %copy-done.6), custom_call_target="tpu_custom_call" | custom-call | flops 10000000000 | bytes 1000000 | tf_op jit(solution)/shard_map/pallas_call | solution.py:204
  10.9 5.1 %all-to-all-start = ((bf16[16,32,128]{2,1,0:T(8,128)(2,1)}), bf16[16,32,128]{2,1,0:T(8,128)(2,1)S(1)}, u32[]{:S(2)}, u32[]{:S(2)}) async-start(bf16[16,32,128]{2,1,0:T(8,128)(2,1)} %shard_map.131), calls=%async_computation | async-start | bytes 262144 | tf_op jit(solution)/shard_map/all_to_all | solution.py:212
  17.3 0.0 copy-done.5
  17.3 0.0 copy-done.4
  17.4 0.0 copy-done.3
  17.4 0.0 copy-done.7
  17.4 0.0 copy-done.8
  17.4 0.0 copy-done.9
  17.4 0.0 copy-start.1
  17.4 0.0 copy-start.2
  17.4 0.1 shard_map.132
  17.5 7.4 %all-to-all-done.query_ref = bf16[16,32,128]{2,1,0:T(8,128)(2,1)S(1)} async-done(((bf16[16,32,128]{2,1,0:T(8,128)(2,1)}), bf16[16,32,128]{2,1,0:T(8,128)(2,1)S(1)}, u32[]{:S(2)}, u32[]{:S(2)}) %all-to-all-start) | async-done | bytes 131104 | tf_op jit(solution)/shard_map/all_to_all | solution.py:212
  24.9 0.0 copy-done.1
  24.9 0.0 copy-done.2
  24.9 0.0 copy-start
  24.9 0.7 %shard_map.133 = bf16[16,18,2,128]{3,2,1,0:T(2,128)(2,1)S(1)} custom-call(s32[1]{0:T(128)} %bitcast.place_ref, bf16[16,32,128]{2,1,0:T(8,128)(2,1)S(1)} %all-to-all-done.query_ref, bf16[128,1024]{1,0:T(8,128)(2,1)S(1)} %copy-done.1, bf16[128,1024]{1,0:T(8,128)(2,1)S(1)} %copy-done.2, bf16[256,1024]{1,0:T(8,128)(2,1)S(1)} %get-tuple-element.6.own_ref, ...), custom_call_target="tpu_custom_call" | custom-call | flops 10000000000 | bytes 1000000 | tf_op jit(solution)/shard_map/pallas_call | solution.py:237
  25.7 12.0 %all_to_all.15.got_ref = bf16[16,18,2,128]{3,2,1,0:T(2,128)(2,1)S(1)} all-to-all(bf16[16,18,2,128]{3,2,1,0:T(2,128)(2,1)S(1)} %shard_map.133), channel_id=1, replica_groups=mesh['dp'=32,'mp'=16] {'mp'}, dimensions={0} | all-to-all | bytes 294912 | tf_op jit(solution)/shard_map/all_to_all | solution.py:246
  37.7 0.0 collective-permute-done.other_hbm
  37.7 0.0 copy-done
  37.7 2.6 %shard_map.134 = bf16[8,64,128]{2,1,0:T(8,128)(2,1)S(1)} custom-call(s32[1]{0:T(128)} %bitcast.place_ref, bf16[16,18,2,128]{3,2,1,0:T(2,128)(2,1)S(1)} %all_to_all.15.got_ref, bf16[256,8192]{1,0:T(8,128)(2,1)S(1)} %copy-done, bf16[256,8192]{1,0:T(8,128)(2,1)} %collective-permute-done.other_hbm), custom_call_target="tpu_custom_call" | custom-call | flops 10000000000 | bytes 1000000 | tf_op jit(solution)/shard_map/pallas_call | solution.py:247
  40.3 10.8 %all_to_all.16.got_ref = bf16[8,64,128]{2,1,0:T(8,128)(2,1)S(1)} all-to-all(bf16[8,64,128]{2,1,0:T(8,128)(2,1)S(1)} %shard_map.134), channel_id=1, replica_groups={{0,2,4,6,8,10,12,14},{1,3,5,7,9,11,13,15},{16,18,20,22,24,26,28,30},{17..., dimensions={0} | all-to-all | bytes 262144 | tf_op jit(solution)/shard_map/all_to_all | solution.py:261
  51.1 0.8 %shard_map.135 = (bf16[1,8192]{1,0:T(2,128)(2,1)}, bf16[1,8192]{1,0:T(2,128)(2,1)}) custom-call(bf16[8,64,128]{2,1,0:T(8,128)(2,1)S(1)} %all_to_all.16.got_ref, f32[64,128]{1,0:T(8,128)S(1)} %get-tuple-element.8.residual_ref, f32[64,128]{1,0:T(8,128)S(1)} %get-tuple-element.9.gain_ref), custom_call_target="tpu_custom_call" | custom-call | tf_op jit(solution)/shard_map/pallas_call | solution.py:263
Async XLA Ops:
  0.6 16.7 %copy-start.5 = (bf16[1,8192]{1,0:T(2,128)(2,1)S(1)}, bf16[1,8192]{1,0:T(2,128)(2,1)}, u32[]{:S(2)}) copy-start(bf16[1,8192]{1,0:T(2,128)(2,1)} %residual_ref.1) | copy-start | bytes 49156
  0.6 16.7 %copy-start.4 = (bf16[1,64,1024]{2,1,0:T(8,128)(2,1)S(1)}, bf16[1,64,1024]{2,1,0:T(8,128)(2,1)}, u32[]{:S(2)}) copy-start(bf16[1,64,1024]{2,1,0:T(8,128)(2,1)} %svalues_ref.1) | copy-start | bytes 393220
  0.7 16.7 %copy-start.3 = (bf16[1,64,1024]{2,1,0:T(8,128)(2,1)S(1)}, bf16[1,64,1024]{2,1,0:T(8,128)(2,1)}, u32[]{:S(2)}) copy-start(bf16[1,64,1024]{2,1,0:T(8,128)(2,1)} %skeys_ref.1) | copy-start | bytes 393220
  0.7 37.0 %collective-permute-start = (bf16[256,8192]{1,0:T(8,128)(2,1)}, bf16[256,8192]{1,0:T(8,128)(2,1)}, u32[]{:S(2)}, u32[]{:S(2)}) collective-permute-start(bf16[256,8192]{1,0:T(8,128)(2,1)} %own_ref.1), channel_id=1, source_target_pairs={{0,1},{1,0},{2,3},{3,2},{4,5},{5,4},{6,7},{7,6},{8,9},{9,8},{10,11... | collective-permute-start | bytes 12582920 | tf_op jit(solution)/shard_map/ppermute | solution.py:236
  9.6 0.7 %copy-start.6 = (bf16[1,4096]{1,0:T(2,128)(2,1)S(1)}, bf16[1,4096]{1,0:T(2,128)(2,1)}, u32[]{:S(2)}) copy-start(bf16[1,4096]{1,0:T(2,128)(2,1)} %query_ref.1) | copy-start | bytes 24580
  10.3 7.1 %copy-start.7 = (bf16[8192]{0:T(1024)(128)(2,1)S(1)}, bf16[8192]{0:T(1024)(128)(2,1)}, u32[]{:S(2)}) copy-start(bf16[8192]{0:T(1024)(128)(2,1)} %param.23) | copy-start | bytes 49156
  10.3 7.1 %copy-start.8 = (bf16[1,1024]{1,0:T(2,128)(2,1)S(1)}, bf16[1,1024]{1,0:T(2,128)(2,1)}, u32[]{:S(2)}) copy-start(bf16[1,1024]{1,0:T(2,128)(2,1)} %key_ref.1) | copy-start | bytes 6148
  10.3 7.1 %copy-start.9 = (bf16[1,1024]{1,0:T(2,128)(2,1)S(1)}, bf16[1,1024]{1,0:T(2,128)(2,1)}, u32[]{:S(2)}) copy-start(bf16[1,1024]{1,0:T(2,128)(2,1)} %value_ref.1) | copy-start | bytes 6148
  10.9 14.0 %all-to-all-start = ((bf16[16,32,128]{2,1,0:T(8,128)(2,1)}), bf16[16,32,128]{2,1,0:T(8,128)(2,1)S(1)}, u32[]{:S(2)}, u32[]{:S(2)}) async-start(bf16[16,32,128]{2,1,0:T(8,128)(2,1)} %shard_map.131), calls=%async_computation | async-start | bytes 262144 | tf_op jit(solution)/shard_map/all_to_all | solution.py:212
  17.4 7.5 %copy-start.1 = (bf16[128,1024]{1,0:T(8,128)(2,1)S(1)}, bf16[128,1024]{1,0:T(8,128)(2,1)}, u32[]{:S(2)}) copy-start(bf16[128,1024]{1,0:T(8,128)(2,1)} %pkeys_ref.1) | copy-start | bytes 786436
  17.4 7.5 %copy-start.2 = (bf16[128,1024]{1,0:T(8,128)(2,1)S(1)}, bf16[128,1024]{1,0:T(8,128)(2,1)}, u32[]{:S(2)}) copy-start(bf16[128,1024]{1,0:T(8,128)(2,1)} %pvalues_ref.1) | copy-start | bytes 786436
  24.9 12.8 %copy-start = (bf16[256,8192]{1,0:T(8,128)(2,1)S(1)}, bf16[256,8192]{1,0:T(8,128)(2,1)}, u32[]{:S(2)}) copy-start(bf16[256,8192]{1,0:T(8,128)(2,1)} %own_ref.1) | copy-start | bytes 12582916

commit v4 on v3

v4 whole, which is shorter than its diff:
```python
import jax
import jax.numpy as jnp
from jax import lax
from jax.experimental import pallas as pl
from jax.experimental.pallas import tpu as pltpu
from jax.sharding import PartitionSpec as P


HEAD_SIZE = 128
KEY_VALUE_HEADS = 8
HQ = 32
GROUP = HQ // KEY_VALUE_HEADS
SAMPLES = 16
CHIPS = 8
D = 8192
BLOCKS = D // 128
WIDTH = 1024
ROWS = 10
SCALE = HEAD_SIZE ** (-0.5)
MASKED = -1e30
LOWEST = -1e29
F32 = jnp.float32
BF16 = jnp.bfloat16

LONG = pl.CostEstimate(flops=10**10, bytes_accessed=10**6, transcendentals=0)


def vmem(count):
    return [pl.BlockSpec(memory_space=pltpu.VMEM)] * count


def at_most(mebibytes):
    return pltpu.CompilerParams(vmem_limit_bytes=mebibytes * 2**20)


def smem(count):
    return [pl.BlockSpec(memory_space=pltpu.SMEM)] * count


def spread_kernel(query_ref, out_ref):
    rows = [query_ref[0:1, h * 128 : (h + 1) * 128].astype(F32) for h in range(HQ)]
    rows = jnp.concatenate(rows, axis=0).astype(BF16)
    for i in range(CHIPS):
        out_ref[i] = rows


def pair_kernel(pkeys_ref, pvalues_ref, prefix_ref):
    prefix_ref[:128] = pkeys_ref[...]
    prefix_ref[128:] = pvalues_ref[...]


def stage_kernel(
    place_ref,
    prefix_len_ref,
    suffix_len_ref,
    skeys_ref,
    svalues_ref,
    key_ref,
    value_ref,
    residual_ref,
    gain_ref,
    own_ref,
    bias_ref,
    residual_rows_ref,
    gain_rows_ref,
):
    first = lax.broadcasted_iota(jnp.int32, (64, 1024), 0) == 0
    own_ref[0:64] = skeys_ref[0]
    own_ref[64:128] = jnp.where(first, key_ref[...].astype(F32), 0.0).astype(BF16)
    own_ref[128:192] = svalues_ref[0]
    own_ref[192:256] = jnp.where(first, value_ref[...].astype(F32), 0.0).astype(BF16)
    rows = [residual_ref[0:1, 128 * i : 128 * i + 128].astype(F32) for i in range(BLOCKS)]
    residual_rows_ref[...] = jnp.concatenate(rows, axis=0)
    gain_rows_ref[...] = gain_ref[...].astype(F32)
    place = place_ref[0]
    row = lax.broadcasted_iota(jnp.int32, (32, 128), 0)
    lane = lax.broadcasted_iota(jnp.int32, (32, 128), 1)
    prefix_len = prefix_len_ref[0]
    other_place = place + 1 - 2 * (place % 2)
    own = (row % 8 == place // 2) & ((lane < suffix_len_ref[0]) | (lane == 64))
    seen = (lane + place * 128 < prefix_len, lane + other_place * 128 < prefix_len, own)
    for i, mask in enumerate(seen):
        bias_ref[i] = jnp.where(mask, 0.0, MASKED)


def attend_kernel(
    place_ref,
    query_ref,
    prefix_ref,
    other_ref,
    own_ref,
    bias_ref,
    out_ref,
    queries,
):
    queries[...] = query_ref[...].reshape(CHIPS * HQ, 128).astype(F32)
    row = lax.broadcasted_iota(jnp.int32, (32, 128), 0)
    lane = lax.broadcasted_iota(jnp.int32, (32, 128), 1)
    mark = lane == row % 16 + 16 * (place_ref[0] // 2)
    ones = jnp.ones((384, 128), BF16)
    zeros = jnp.zeros((1, 128), F32)
    heads = [slice(k * 128, (k + 1) * 128) for k in range(KEY_VALUE_HEADS)]
    parts = (prefix_ref, other_ref, own_ref)
    scores = []
    for k, head in enumerate(heads):
        query = [queries[pl.ds(k * GROUP + g, 8, stride=HQ), :] for g in range(GROUP)]
        query = jnp.concatenate(query, axis=0).astype(BF16)
        keys = jnp.concatenate([part[:128, head] for part in parts], axis=0)
        product = lax.dot_general(
            query, keys, (((1,), (1,)), ((), ())), preferred_element_type=F32
        )
        scores.append(
            [product[:, 128 * i : 128 * i + 128] * SCALE + bias_ref[i] for i in range(3)]
        )
    tops = [jnp.maximum(jnp.maximum(s[0], s[1]), s[2]) for s in scores]
    tops = [jnp.max(top, axis=-1, keepdims=True) for top in tops]
    tops = [jnp.maximum(top, LOWEST).astype(BF16).astype(F32) for top in tops]
    weights = [
        jnp.concatenate([jnp.exp(s - top) for s in three], axis=1).astype(BF16)
        for three, top in zip(scores, tops)
    ]
    summed = []
    for weight, head in zip(weights, heads):
        values = jnp.concatenate([part[128:, head] for part in parts], axis=0)
        values = jnp.concatenate([values, ones], axis=1)
        summed.append(jnp.dot(weight, values, preferred_element_type=F32))
    for k, (top, sums) in enumerate(zip(tops, summed)):
        total_high = sums[:, 128:].astype(BF16).astype(F32)
        total_low = sums[:, 128:] - total_high
        for c in range(2):
            part = slice(16 * c, 16 * c + 16)
            out_ref[2 * k + c, 0:8] = sums[part, :128].astype(BF16).reshape(8, 2, 128)
            stats = [
                jnp.sum(jnp.where(mark[part], v[part], 0.0), axis=0, keepdims=True)
                for v in (top, total_high, total_low)
            ]
            stats = jnp.concatenate(stats + [zeros], axis=0).astype(BF16)
            out_ref[2 * k + c, 8:ROWS] = stats.reshape(2, 2, 128)


def project_kernel(place_ref, got_ref, weight_ref, out_ref, rows):
    row = lax.broadcasted_iota(jnp.int32, (16, 128), 0)
    lane = lax.broadcasted_iota(jnp.int32, (16, 128), 1)
    diagonal = lane % 16 == row
    joined = []
    for c in range(2):
        sources = range(c, SAMPLES, 2)
        stats = sum(got_ref[i, 8:ROWS].reshape(4, 128).astype(F32) for i in sources)
        tops, totals = stats[0:1], stats[1:2] + stats[2:3]
        top = tops
        for shift in (64, 32, 16):
            top = jnp.maximum(top, pltpu.roll(top, shift, 1))
        factors = jnp.exp(tops - top)
        total = factors * totals
        for shift in (64, 32, 16):
            total = total + pltpu.roll(total, shift, 1)
        mix = jnp.where(diagonal, factors / total, 0.0)
        high = mix.astype(BF16)
        low = (mix - high.astype(F32)).astype(BF16)
        sums = jnp.concatenate([got_ref[i, 0:8].reshape(16, 128) for i in sources], axis=0)
        both = jnp.dot(jnp.concatenate([high, low], axis=0), sums, preferred_element_type=F32)
        joined.append(both[:16] + both[16:])
    attn = [jnp.concatenate([a[8 * g : 8 * g + 8] for a in joined], axis=0) for g in range(2)]
    attn = jnp.concatenate(attn, axis=1).astype(BF16)
    for n in range(0, D, WIDTH):
        piece = jnp.dot(attn, weight_ref[:, n : n + WIDTH], preferred_element_type=F32)
        for i in range(WIDTH // 128):
            for c in range(2):
                rows[pl.ds(c * BLOCKS + n // 128 + i, 8, stride=2 * BLOCKS), :] = piece[
                    8 * c : 8 * c + 8, 128 * i : 128 * i + 128
                ]
    out_ref[...] = rows[...].astype(BF16).reshape(SAMPLES, BLOCKS, 128)


def finish_kernel(got_ref, residual_ref, gain_ref, hidden_ref, normed_ref):
    proj = got_ref[0].astype(F32)
    for i in range(1, SAMPLES):
        proj += got_ref[i].astype(F32)
    stream = residual_ref[...] + proj
    scale = lax.rsqrt(jnp.sum(stream * stream) * (1.0 / D) + 1e-05)
    normed = stream * scale * gain_ref[...]
    for i in range(BLOCKS):
        cols = slice(128 * i, 128 * i + 128)
        hidden_ref[0:1, cols] = stream[i : i + 1].astype(BF16)
        normed_ref[0:1, cols] = normed[i : i + 1].astype(BF16)


def local(
    query_new,
    key_new,
    value_new,
    prefix_keys,
    prefix_values,
    sample_suffix_keys,
    sample_suffix_values,
    prefix_len,
    suffix_len,
    residual,
    out_weight,
    norm_gain,
):
    place = lax.axis_index("mp").astype(jnp.int32)[None]
    cores = [[2 * z + c for z in range(CHIPS)] for c in range(2)]
    spread = pl.pallas_call(
        spread_kernel,
        out_shape=jax.ShapeDtypeStruct((CHIPS, HQ, 128), BF16),
        in_specs=vmem(1),
        out_specs=vmem(1)[0],
        compiler_params=at_most(2),
        cost_estimate=LONG,
    )(query_new)
    queries = lax.all_to_all(spread, "mp", 0, 0, tiled=True, axis_index_groups=cores)
    prefix = pl.pallas_call(
        pair_kernel,
        out_shape=jax.ShapeDtypeStruct((256, 1024), BF16),
        in_specs=vmem(2),
        out_specs=vmem(1)[0],
        compiler_params=at_most(2),
        cost_estimate=LONG,
    )(prefix_keys, prefix_values)
    other_prefix = lax.ppermute(prefix, "mp", [(i, i ^ 1) for i in range(SAMPLES)])
    own, bias, residual_rows, gain_rows = pl.pallas_call(
        stage_kernel,
        out_shape=[
            jax.ShapeDtypeStruct((256, 1024), BF16),
            jax.ShapeDtypeStruct((3, 32, 128), F32),
            jax.ShapeDtypeStruct((BLOCKS, 128), F32),
            jax.ShapeDtypeStruct((BLOCKS, 128), F32),
        ],
        in_specs=smem(3) + vmem(6),
        out_specs=vmem(4),
        compiler_params=at_most(4),
        cost_estimate=LONG,
    )(
        place,
        prefix_len,
        suffix_len,
        sample_suffix_keys,
        sample_suffix_values,
        key_new,
        value_new,
        residual,
        norm_gain.reshape(BLOCKS, 128),
    )
    partial = pl.pallas_call(
        attend_kernel,
        out_shape=jax.ShapeDtypeStruct((SAMPLES, ROWS, 2, 128), BF16),
        in_specs=smem(1) + vmem(5),
        out_specs=vmem(1)[0],
        scratch_shapes=[pltpu.VMEM((CHIPS * HQ, 128), F32)],
        compiler_params=at_most(8),
        cost_estimate=LONG,
    )(place, queries, prefix, other_prefix, own, bias)
    partial = lax.all_to_all(partial, "mp", 0, 0, tiled=True)
    proj = pl.pallas_call(
        project_kernel,
        out_shape=jax.ShapeDtypeStruct((SAMPLES, BLOCKS, 128), BF16),
        in_specs=smem(1) + vmem(2),
        out_specs=vmem(1)[0],
        scratch_shapes=[pltpu.VMEM((SAMPLES * BLOCKS, 128), F32)],
        compiler_params=at_most(12),
        cost_estimate=LONG,
    )(place, partial, out_weight)
    proj = lax.all_to_all(proj, "mp", 0, 0, tiled=True)
    return tuple(
        pl.pallas_call(
            finish_kernel,
            out_shape=[jax.ShapeDtypeStruct((1, D), BF16)] * 2,
            in_specs=vmem(3),
            out_specs=vmem(2),
            compiler_params=at_most(4),
        )(proj, residual_rows, gain_rows)
    )


def solution(mesh):
    whole = P(("dp", "mp"), None)
    placed = (
        whole,
        whole,
        whole,
        whole,
        whole,
        P(("dp", "mp"), None, None),
        P(("dp", "mp"), None, None),
        P("dp"),
        P(("dp", "mp")),
        whole,
        P("mp", None),
        P(),
    )

    def step(*arrays):
        return local(*arrays)

    step = jax.shard_map(
        step, mesh=mesh, in_specs=placed, out_specs=(whole, whole), check_vma=False
    )
    return step
```

time: 52.4 us -> 50.5 us (0.964)
  waiting for transfers between devices: 7.43 us -> 2.67 us
  blocking collectives: 22.9 us -> 27.1 us
  Pallas kernels: 4.85 us -> 3.55 us
    ppermute x1, starting transfers between devices: 8.88 us -> 3 us  [local(): lax.ppermute(prefix, 'mp', [(i, i ^ 1) for i in range(SAMPLES)])]
    all_to_all x1, starting transfers between devices: 5.1 us -> 10.9 us  [local(): lax.all_to_all(spread, 'mp', 0, 0, tiled=True, axis_index_groups=cores)]
    all_to_all x1, waiting for transfers between devices: 7.43 us -> 2.67 us  [local(): lax.all_to_all(spread, 'mp', 0, 0, tiled=True, axis_index_groups=cores)]
    all_to_all x1, blocking collectives: 10.8 us -> 14.1 us  [local(): proj = lax.all_to_all(proj, 'mp', 0, 0, tiled=True)]
    pallas_call x2 -> x3, Pallas kernels: 3.23 us -> 1.95 us  [the longest x1 1.27 us: local(): pl.pallas_call(project_kernel, out_shape=jax.ShapeDtypeStruct((SAMPLES, B...]
    all_to_all x1, blocking collectives: 12 us -> 13 us  [local(): partial = lax.all_to_all(partial, 'mp', 0, 0, tiled=True)]
  transfers between devices with their start and end apart: 2 -> 2, of which waited for: 1 -> 1; matrix products, arithmetic and copies ran while one was open for 0% -> 0% of each run, Pallas kernels for 3% -> 0%
where the time goes in v4:
time: 50.5 us; the launch traced here: 50.1 us
  blocking collectives  27.1 us (54%)
  starting transfers between devices  13.8 us (27%)
  Pallas kernels  3.55 us (7%)
  waiting for transfers between devices  2.67 us (5%)
  between operations  2.1 us (4%)
  local copies, waits for them, and re-layouts  0.82 us (2%)
    all_to_all x1, blocking collectives, local(): proj = lax.all_to_all(proj, 'mp', 0, 0, tiled=True)  14.1 us
    all_to_all x1, blocking collectives, local(): partial = lax.all_to_all(partial, 'mp', 0, 0, tiled=True)  13 us
    all_to_all x1, starting transfers between devices, local(): lax.all_to_all(spread, 'mp', 0, 0, tiled=True, axis_index_groups=cores)  10.9 us
    ppermute x1, starting transfers between devices, local(): lax.ppermute(prefix, 'mp', [(i, i ^ 1) for i in range(SAMPLES)])  3 us
    all_to_all x1, waiting for transfers between devices, local(): lax.all_to_all(spread, 'mp', 0, 0, tiled=True, axis_index_groups=cores)  2.67 us
    pallas_call x1, Pallas kernels, local(): pl.pallas_call(project_kernel, out_shape=jax.ShapeDtypeStruct((SAMPLES, B...  1.27 us
  transfers between devices with their start and end apart: 2, of which 1 were waited for; matrix products, arithmetic and copies ran while one was open for 0% of the time, Pallas kernels for 0%

profile of v4, /device:TPU:1, one launch (start us, length us, event | category | flops | bytes accessed | tf_op | source)
XLA Modules:
  0.0 50.1 jit_solution(15186040140090881378)
XLA Ops:
  0.6 0.0 copy-start.2
  0.6 0.0 copy-start.1
  0.6 0.0 copy-start.6
  0.7 0.8 %copy-done.6 = bf16[1,4096]{1,0:T(2,128)(2,1)S(1)} copy-done((bf16[1,4096]{1,0:T(2,128)(2,1)S(1)}, bf16[1,4096]{1,0:T(2,128)(2,1)}, u32[]{:S(2)}) %copy-start.6) | copy-done | bytes 8216
  1.4 0.6 %shard_map.131 = bf16[8,32,128]{2,1,0:T(8,128)(2,1)} custom-call(bf16[1,4096]{1,0:T(2,128)(2,1)S(1)} %copy-done.6), custom_call_target="tpu_custom_call" | custom-call | flops 10000000000 | bytes 1000000 | tf_op jit(solution)/shard_map/pallas_call | solution.py:204
  2.1 10.9 %all-to-all-start = ((bf16[8,32,128]{2,1,0:T(8,128)(2,1)}), bf16[8,32,128]{2,1,0:T(8,128)(2,1)S(1)}, u32[]{:S(2)}, u32[]{:S(2)}) async-start(bf16[8,32,128]{2,1,0:T(8,128)(2,1)} %shard_map.131), calls=%async_computation | async-start | bytes 131072 | tf_op jit(solution)/shard_map/all_to_all | solution.py:212
  12.9 0.0 copy-done.2
  12.9 0.0 copy-done.1
  12.9 0.0 copy-start.3
  12.9 0.0 copy-start.4
  13.0 0.0 copy-start.5
  13.0 0.0 copy-start.7
  13.0 0.0 copy-start.8
  13.0 0.0 copy-start.9
  13.1 3.0 %collective-permute-start = (bf16[256,1024]{1,0:T(8,128)(2,1)S(1)}, bf16[256,1024]{1,0:T(8,128)(2,1)S(1)}, u32[]{:S(2)}, u32[]{:S(2)}) collective-permute-start(bf16[256,1024]{1,0:T(8,128)(2,1)S(1)} %shard_map.132.prefix_ref), channel_id=1, source_target_pairs={{0,1},{1,0},{2,3},{3,2},{4,5},{5,4},{6,7},{7,6},{8,9},{9,8},{10,11... | collective-permute-start | bytes 1572872 | tf_op jit(solution)/shard_map/ppermute | solution.py:221
  17.4 0.0 copy-done.3
  17.4 0.0 copy-done.4
  17.4 0.0 copy-done.5
  17.4 0.0 copy-done.7
  17.4 0.0 copy-done.8
  17.4 0.0 copy-done.9
  17.4 0.1 shard_map.133
  17.5 2.7 %all-to-all-done.query_ref = bf16[8,32,128]{2,1,0:T(8,128)(2,1)S(1)} async-done(((bf16[8,32,128]{2,1,0:T(8,128)(2,1)}), bf16[8,32,128]{2,1,0:T(8,128)(2,1)S(1)}, u32[]{:S(2)}, u32[]{:S(2)}) %all-to-all-start) | async-done | bytes 65568 | tf_op jit(solution)/shard_map/all_to_all | solution.py:212
  20.2 0.0 collective-permute-done.other_ref
  20.2 0.0 copy-start
  20.2 0.7 %shard_map.134 = bf16[16,10,2,128]{3,2,1,0:T(2,128)(2,1)S(1)} custom-call(s32[1]{0:T(128)} %bitcast.place_ref, bf16[8,32,128]{2,1,0:T(8,128)(2,1)S(1)} %all-to-all-done.query_ref, bf16[256,1024]{1,0:T(8,128)(2,1)S(1)} %shard_map.132.prefix_ref, bf16[256,1024]{1,0:T(8,128)(2,1)S(1)} %collective-permute-done.other_ref, ...), custom_call_target="tpu_custom_call" | custom-call | flops 10000000000 | bytes 1000000 | tf_op jit(solution)/shard_map/pallas_call | solution.py:245
  20.9 13.0 %all_to_all.15.got_ref = bf16[16,10,2,128]{3,2,1,0:T(2,128)(2,1)S(1)} all-to-all(bf16[16,10,2,128]{3,2,1,0:T(2,128)(2,1)S(1)} %shard_map.134), channel_id=1, replica_groups=mesh['dp'=32,'mp'=16] {'mp'}, dimensions={0} | all-to-all | bytes 163840 | tf_op jit(solution)/shard_map/all_to_all | solution.py:254
  33.9 0.0 copy-done
  33.9 1.3 %shard_map.135 = bf16[16,64,128]{2,1,0:T(8,128)(2,1)S(1)} custom-call(s32[1]{0:T(128)} %bitcast.place_ref, bf16[16,10,2,128]{3,2,1,0:T(2,128)(2,1)S(1)} %all_to_all.15.got_ref, bf16[256,8192]{1,0:T(8,128)(2,1)S(1)} %copy-done), custom_call_target="tpu_custom_call" | custom-call | flops 10000000000 | bytes 1000000 | tf_op jit(solution)/shard_map/pallas_call | solution.py:255
  35.2 14.1 %all_to_all.16.got_ref = bf16[16,64,128]{2,1,0:T(8,128)(2,1)S(1)} all-to-all(bf16[16,64,128]{2,1,0:T(8,128)(2,1)S(1)} %shard_map.135), channel_id=1, replica_groups=mesh['dp'=32,'mp'=16] {'mp'}, dimensions={0} | all-to-all | bytes 524288 | tf_op jit(solution)/shard_map/all_to_all | solution.py:264
  49.3 0.8 %shard_map.136 = (bf16[1,8192]{1,0:T(2,128)(2,1)}, bf16[1,8192]{1,0:T(2,128)(2,1)}) custom-call(bf16[16,64,128]{2,1,0:T(8,128)(2,1)S(1)} %all_to_all.16.got_ref, f32[64,128]{1,0:T(8,128)S(1)} %get-tuple-element.8.residual_ref, f32[64,128]{1,0:T(8,128)S(1)} %get-tuple-element.9.gain_ref), custom_call_target="tpu_custom_call" | custom-call | tf_op jit(solution)/shard_map/pallas_call | solution.py:266
  (1 shorter events, 0.0 us)
Async XLA Ops:
  0.6 12.3 %copy-start.2 = (bf16[128,1024]{1,0:T(8,128)(2,1)S(1)}, bf16[128,1024]{1,0:T(8,128)(2,1)}, u32[]{:S(2)}) copy-start(bf16[128,1024]{1,0:T(8,128)(2,1)} %pvalues_ref.1) | copy-start | bytes 786436
  0.6 12.3 %copy-start.1 = (bf16[128,1024]{1,0:T(8,128)(2,1)S(1)}, bf16[128,1024]{1,0:T(8,128)(2,1)}, u32[]{:S(2)}) copy-start(bf16[128,1024]{1,0:T(8,128)(2,1)} %pkeys_ref.1) | copy-start | bytes 786436
  0.6 0.8 %copy-start.6 = (bf16[1,4096]{1,0:T(2,128)(2,1)S(1)}, bf16[1,4096]{1,0:T(2,128)(2,1)}, u32[]{:S(2)}) copy-start(bf16[1,4096]{1,0:T(2,128)(2,1)} %query_ref.1) | copy-start | bytes 24580
  2.1 18.1 %all-to-all-start = ((bf16[8,32,128]{2,1,0:T(8,128)(2,1)}), bf16[8,32,128]{2,1,0:T(8,128)(2,1)S(1)}, u32[]{:S(2)}, u32[]{:S(2)}) async-start(bf16[8,32,128]{2,1,0:T(8,128)(2,1)} %shard_map.131), calls=%async_computation | async-start | bytes 131072 | tf_op jit(solution)/shard_map/all_to_all | solution.py:212
  12.9 4.4 %copy-start.3 = (bf16[1,64,1024]{2,1,0:T(8,128)(2,1)S(1)}, bf16[1,64,1024]{2,1,0:T(8,128)(2,1)}, u32[]{:S(2)}) copy-start(bf16[1,64,1024]{2,1,0:T(8,128)(2,1)} %skeys_ref.1) | copy-start | bytes 393220
  12.9 4.4 %copy-start.4 = (bf16[1,64,1024]{2,1,0:T(8,128)(2,1)S(1)}, bf16[1,64,1024]{2,1,0:T(8,128)(2,1)}, u32[]{:S(2)}) copy-start(bf16[1,64,1024]{2,1,0:T(8,128)(2,1)} %svalues_ref.1) | copy-start | bytes 393220
  13.0 4.4 %copy-start.5 = (bf16[1,8192]{1,0:T(2,128)(2,1)S(1)}, bf16[1,8192]{1,0:T(2,128)(2,1)}, u32[]{:S(2)}) copy-start(bf16[1,8192]{1,0:T(2,128)(2,1)} %residual_ref.1) | copy-start | bytes 49156
  13.0 4.4 %copy-start.7 = (bf16[8192]{0:T(1024)(128)(2,1)S(1)}, bf16[8192]{0:T(1024)(128)(2,1)}, u32[]{:S(2)}) copy-start(bf16[8192]{0:T(1024)(128)(2,1)} %param.23) | copy-start | bytes 49156
  13.0 4.4 %copy-start.8 = (bf16[1,1024]{1,0:T(2,128)(2,1)S(1)}, bf16[1,1024]{1,0:T(2,128)(2,1)}, u32[]{:S(2)}) copy-start(bf16[1,1024]{1,0:T(2,128)(2,1)} %key_ref.1) | copy-start | bytes 6148
  13.0 4.4 %copy-start.9 = (bf16[1,1024]{1,0:T(2,128)(2,1)S(1)}, bf16[1,1024]{1,0:T(2,128)(2,1)}, u32[]{:S(2)}) copy-start(bf16[1,1024]{1,0:T(2,128)(2,1)} %value_ref.1) | copy-start | bytes 6148
  13.1 7.1 %collective-permute-start = (bf16[256,1024]{1,0:T(8,128)(2,1)S(1)}, bf16[256,1024]{1,0:T(8,128)(2,1)S(1)}, u32[]{:S(2)}, u32[]{:S(2)}) collective-permute-start(bf16[256,1024]{1,0:T(8,128)(2,1)S(1)} %shard_map.132.prefix_ref), channel_id=1, source_target_pairs={{0,1},{1,0},{2,3},{3,2},{4,5},{5,4},{6,7},{7,6},{8,9},{9,8},{10,11... | collective-permute-start | bytes 1572872 | tf_op jit(solution)/shard_map/ppermute | solution.py:221
  20.2 13.7 %copy-start = (bf16[256,8192]{1,0:T(8,128)(2,1)S(1)}, bf16[256,8192]{1,0:T(8,128)(2,1)}, u32[]{:S(2)}) copy-start(bf16[256,8192]{1,0:T(8,128)(2,1)} %weight_ref.1) | copy-start | bytes 12582916

commit v5 on v4

--- a/solution.py
+++ b/solution.py
@@ -142,24 +142,30 @@
     row = lax.broadcasted_iota(jnp.int32, (16, 128), 0)
     lane = lax.broadcasted_iota(jnp.int32, (16, 128), 1)
     diagonal = lane % 16 == row
+    stats = [
+        sum(got_ref[i, 8:ROWS].reshape(4, 128).astype(F32) for i in range(c, SAMPLES, 2))
+        for c in range(2)
+    ]
+    tops = jnp.concatenate([s[0:1] for s in stats], axis=0)
+    totals = jnp.concatenate([s[1:2] + s[2:3] for s in stats], axis=0)
+    top = tops
+    for shift in (64, 32, 16):
+        top = jnp.maximum(top, pltpu.roll(top, shift, 1))
+    factors = jnp.exp(tops - top)
+    total = factors * totals
+    for shift in (64, 32, 16):
+        total = total + pltpu.roll(total, shift, 1)
+    factors = factors / total
+    mixes = [jnp.where(diagonal, factors[c : c + 1], 0.0) for c in range(2)]
+    highs = [mix.astype(BF16) for mix in mixes]
+    lows = [(mix - high.astype(F32)).astype(BF16) for mix, high in zip(mixes, highs)]
     joined = []
     for c in range(2):
-        sources = range(c, SAMPLES, 2)
-        stats = sum(got_ref[i, 8:ROWS].reshape(4, 128).astype(F32) for i in sources)
-        tops, totals = stats[0:1], stats[1:2] + stats[2:3]
-        top = tops
-        for shift in (64, 32, 16):
-            top = jnp.maximum(top, pltpu.roll(top, shift, 1))
-        factors = jnp.exp(tops - top)
-        total = factors * totals
-        for shift in (64, 32, 16):
-            total = total + pltpu.roll(total, shift, 1)
-        mix = jnp.where(diagonal, factors / total, 0.0)
-        high = mix.astype(BF16)
-        low = (mix - high.astype(F32)).astype(BF16)
-        sums = jnp.concatenate([got_ref[i, 0:8].reshape(16, 128) for i in sources], axis=0)
-        both = jnp.dot(jnp.concatenate([high, low], axis=0), sums, preferred_element_type=F32)
-        joined.append(both[:16] + both[16:])
+        sums = [got_ref[i, 0:8].reshape(16, 128) for i in range(c, SAMPLES, 2)]
+        sums = jnp.concatenate(sums, axis=0)
+        both = jnp.concatenate([highs[c], lows[c]], axis=0)
+        joined.append(jnp.dot(both, sums, preferred_element_type=F32))
+    joined = [both[:16] + both[16:] for both in joined]
     attn = [jnp.concatenate([a[8 * g : 8 * g + 8] for a in joined], axis=0) for g in range(2)]
     attn = jnp.concatenate(attn, axis=1).astype(BF16)
     for n in range(0, D, WIDTH):

time: 50.5 us -> 50.5 us (level)
  no operation moved by 1% of the time
where the time goes in v5:
time: 50.5 us; the launch traced here: 50.1 us
  blocking collectives  27.1 us (54%)
  starting transfers between devices  13.8 us (27%)
  Pallas kernels  3.56 us (7%)
  waiting for transfers between devices  2.67 us (5%)
  between operations  2.1 us (4%)
  local copies, waits for them, and re-layouts  0.82 us (2%)
    all_to_all x1, blocking collectives, local(): proj = lax.all_to_all(proj, 'mp', 0, 0, tiled=True)  14.1 us
    all_to_all x1, blocking collectives, local(): partial = lax.all_to_all(partial, 'mp', 0, 0, tiled=True)  13 us
    all_to_all x1, starting transfers between devices, local(): lax.all_to_all(spread, 'mp', 0, 0, tiled=True, axis_index_groups=cores)  10.9 us
    ppermute x1, starting transfers between devices, local(): lax.ppermute(prefix, 'mp', [(i, i ^ 1) for i in range(SAMPLES)])  3 us
    all_to_all x1, waiting for transfers between devices, local(): lax.all_to_all(spread, 'mp', 0, 0, tiled=True, axis_index_groups=cores)  2.67 us
    pallas_call x1, Pallas kernels, local(): pl.pallas_call(project_kernel, out_shape=jax.ShapeDtypeStruct((SAMPLES, B...  1.27 us
  transfers between devices with their start and end apart: 2, of which 1 were waited for; matrix products, arithmetic and copies ran while one was open for 0% of the time, Pallas kernels for 0%

profile of v5, /device:TPU:1, one launch (start us, length us, event | category | flops | bytes accessed | tf_op | source)
XLA Modules:
  0.0 50.1 jit_solution(9665113785281210322)
XLA Ops:
  0.6 0.0 copy-start.2
  0.6 0.0 copy-start.1
  0.6 0.0 copy-start.6
  0.7 0.8 %copy-done.6 = bf16[1,4096]{1,0:T(2,128)(2,1)S(1)} copy-done((bf16[1,4096]{1,0:T(2,128)(2,1)S(1)}, bf16[1,4096]{1,0:T(2,128)(2,1)}, u32[]{:S(2)}) %copy-start.6) | copy-done | bytes 8216
  1.4 0.6 %shard_map.131 = bf16[8,32,128]{2,1,0:T(8,128)(2,1)} custom-call(bf16[1,4096]{1,0:T(2,128)(2,1)S(1)} %copy-done.6), custom_call_target="tpu_custom_call" | custom-call | flops 10000000000 | bytes 1000000 | tf_op jit(solution)/shard_map/pallas_call | solution.py:210
  2.1 10.9 %all-to-all-start = ((bf16[8,32,128]{2,1,0:T(8,128)(2,1)}), bf16[8,32,128]{2,1,0:T(8,128)(2,1)S(1)}, u32[]{:S(2)}, u32[]{:S(2)}) async-start(bf16[8,32,128]{2,1,0:T(8,128)(2,1)} %shard_map.131), calls=%async_computation | async-start | bytes 131072 | tf_op jit(solution)/shard_map/all_to_all | solution.py:218
  12.9 0.0 copy-done.2
  12.9 0.0 copy-done.1
  12.9 0.0 copy-start.3
  12.9 0.0 copy-start.4
  13.0 0.0 copy-start.5
  13.0 0.0 copy-start.7
  13.0 0.0 copy-start.8
  13.0 0.0 copy-start.9
  13.1 3.0 %collective-permute-start = (bf16[256,1024]{1,0:T(8,128)(2,1)S(1)}, bf16[256,1024]{1,0:T(8,128)(2,1)S(1)}, u32[]{:S(2)}, u32[]{:S(2)}) collective-permute-start(bf16[256,1024]{1,0:T(8,128)(2,1)S(1)} %shard_map.132.prefix_ref), channel_id=1, source_target_pairs={{0,1},{1,0},{2,3},{3,2},{4,5},{5,4},{6,7},{7,6},{8,9},{9,8},{10,11... | collective-permute-start | bytes 1572872 | tf_op jit(solution)/shard_map/ppermute | solution.py:227
  17.4 0.0 copy-done.3
  17.4 0.0 copy-done.4
  17.4 0.0 copy-done.5
  17.4 0.0 copy-done.7
  17.4 0.0 copy-done.8
  17.4 0.0 copy-done.9
  17.4 0.1 shard_map.133
  17.5 2.7 %all-to-all-done.query_ref = bf16[8,32,128]{2,1,0:T(8,128)(2,1)S(1)} async-done(((bf16[8,32,128]{2,1,0:T(8,128)(2,1)}), bf16[8,32,128]{2,1,0:T(8,128)(2,1)S(1)}, u32[]{:S(2)}, u32[]{:S(2)}) %all-to-all-start) | async-done | bytes 65568 | tf_op jit(solution)/shard_map/all_to_all | solution.py:218
  20.2 0.0 collective-permute-done.other_ref
  20.2 0.0 copy-start
  20.2 0.7 %shard_map.134 = bf16[16,10,2,128]{3,2,1,0:T(2,128)(2,1)S(1)} custom-call(s32[1]{0:T(128)} %bitcast.place_ref, bf16[8,32,128]{2,1,0:T(8,128)(2,1)S(1)} %all-to-all-done.query_ref, bf16[256,1024]{1,0:T(8,128)(2,1)S(1)} %shard_map.132.prefix_ref, bf16[256,1024]{1,0:T(8,128)(2,1)S(1)} %collective-permute-done.other_ref, ...), custom_call_target="tpu_custom_call" | custom-call | flops 10000000000 | bytes 1000000 | tf_op jit(solution)/shard_map/pallas_call | solution.py:251
  20.9 13.0 %all_to_all.15.got_ref = bf16[16,10,2,128]{3,2,1,0:T(2,128)(2,1)S(1)} all-to-all(bf16[16,10,2,128]{3,2,1,0:T(2,128)(2,1)S(1)} %shard_map.134), channel_id=1, replica_groups=mesh['dp'=32,'mp'=16] {'mp'}, dimensions={0} | all-to-all | bytes 163840 | tf_op jit(solution)/shard_map/all_to_all | solution.py:260
  33.9 0.0 copy-done
  33.9 1.3 %shard_map.135 = bf16[16,64,128]{2,1,0:T(8,128)(2,1)S(1)} custom-call(s32[1]{0:T(128)} %bitcast.place_ref, bf16[16,10,2,128]{3,2,1,0:T(2,128)(2,1)S(1)} %all_to_all.15.got_ref, bf16[256,8192]{1,0:T(8,128)(2,1)S(1)} %copy-done), custom_call_target="tpu_custom_call" | custom-call | flops 10000000000 | bytes 1000000 | tf_op jit(solution)/shard_map/pallas_call | solution.py:261
  35.2 14.1 %all_to_all.16.got_ref = bf16[16,64,128]{2,1,0:T(8,128)(2,1)S(1)} all-to-all(bf16[16,64,128]{2,1,0:T(8,128)(2,1)S(1)} %shard_map.135), channel_id=1, replica_groups=mesh['dp'=32,'mp'=16] {'mp'}, dimensions={0} | all-to-all | bytes 524288 | tf_op jit(solution)/shard_map/all_to_all | solution.py:270
  49.3 0.8 %shard_map.136 = (bf16[1,8192]{1,0:T(2,128)(2,1)}, bf16[1,8192]{1,0:T(2,128)(2,1)}) custom-call(bf16[16,64,128]{2,1,0:T(8,128)(2,1)S(1)} %all_to_all.16.got_ref, f32[64,128]{1,0:T(8,128)S(1)} %get-tuple-element.8.residual_ref, f32[64,128]{1,0:T(8,128)S(1)} %get-tuple-element.9.gain_ref), custom_call_target="tpu_custom_call" | custom-call | tf_op jit(solution)/shard_map/pallas_call | solution.py:272
  (1 shorter events, 0.0 us)
Async XLA Ops:
  0.6 12.3 %copy-start.2 = (bf16[128,1024]{1,0:T(8,128)(2,1)S(1)}, bf16[128,1024]{1,0:T(8,128)(2,1)}, u32[]{:S(2)}) copy-start(bf16[128,1024]{1,0:T(8,128)(2,1)} %pvalues_ref.1) | copy-start | bytes 786436
  0.6 12.3 %copy-start.1 = (bf16[128,1024]{1,0:T(8,128)(2,1)S(1)}, bf16[128,1024]{1,0:T(8,128)(2,1)}, u32[]{:S(2)}) copy-start(bf16[128,1024]{1,0:T(8,128)(2,1)} %pkeys_ref.1) | copy-start | bytes 786436
  0.6 0.8 %copy-start.6 = (bf16[1,4096]{1,0:T(2,128)(2,1)S(1)}, bf16[1,4096]{1,0:T(2,128)(2,1)}, u32[]{:S(2)}) copy-start(bf16[1,4096]{1,0:T(2,128)(2,1)} %query_ref.1) | copy-start | bytes 24580
  2.1 18.1 %all-to-all-start = ((bf16[8,32,128]{2,1,0:T(8,128)(2,1)}), bf16[8,32,128]{2,1,0:T(8,128)(2,1)S(1)}, u32[]{:S(2)}, u32[]{:S(2)}) async-start(bf16[8,32,128]{2,1,0:T(8,128)(2,1)} %shard_map.131), calls=%async_computation | async-start | bytes 131072 | tf_op jit(solution)/shard_map/all_to_all | solution.py:218
  12.9 4.4 %copy-start.3 = (bf16[1,64,1024]{2,1,0:T(8,128)(2,1)S(1)}, bf16[1,64,1024]{2,1,0:T(8,128)(2,1)}, u32[]{:S(2)}) copy-start(bf16[1,64,1024]{2,1,0:T(8,128)(2,1)} %skeys_ref.1) | copy-start | bytes 393220
  12.9 4.4 %copy-start.4 = (bf16[1,64,1024]{2,1,0:T(8,128)(2,1)S(1)}, bf16[1,64,1024]{2,1,0:T(8,128)(2,1)}, u32[]{:S(2)}) copy-start(bf16[1,64,1024]{2,1,0:T(8,128)(2,1)} %svalues_ref.1) | copy-start | bytes 393220
  13.0 4.4 %copy-start.5 = (bf16[1,8192]{1,0:T(2,128)(2,1)S(1)}, bf16[1,8192]{1,0:T(2,128)(2,1)}, u32[]{:S(2)}) copy-start(bf16[1,8192]{1,0:T(2,128)(2,1)} %residual_ref.1) | copy-start | bytes 49156
  13.0 4.4 %copy-start.7 = (bf16[8192]{0:T(1024)(128)(2,1)S(1)}, bf16[8192]{0:T(1024)(128)(2,1)}, u32[]{:S(2)}) copy-start(bf16[8192]{0:T(1024)(128)(2,1)} %param.23) | copy-start | bytes 49156
  13.0 4.4 %copy-start.8 = (bf16[1,1024]{1,0:T(2,128)(2,1)S(1)}, bf16[1,1024]{1,0:T(2,128)(2,1)}, u32[]{:S(2)}) copy-start(bf16[1,1024]{1,0:T(2,128)(2,1)} %key_ref.1) | copy-start | bytes 6148
  13.0 4.4 %copy-start.9 = (bf16[1,1024]{1,0:T(2,128)(2,1)S(1)}, bf16[1,1024]{1,0:T(2,128)(2,1)}, u32[]{:S(2)}) copy-start(bf16[1,1024]{1,0:T(2,128)(2,1)} %value_ref.1) | copy-start | bytes 6148
  13.1 7.1 %collective-permute-start = (bf16[256,1024]{1,0:T(8,128)(2,1)S(1)}, bf16[256,1024]{1,0:T(8,128)(2,1)S(1)}, u32[]{:S(2)}, u32[]{:S(2)}) collective-permute-start(bf16[256,1024]{1,0:T(8,128)(2,1)S(1)} %shard_map.132.prefix_ref), channel_id=1, source_target_pairs={{0,1},{1,0},{2,3},{3,2},{4,5},{5,4},{6,7},{7,6},{8,9},{9,8},{10,11... | collective-permute-start | bytes 1572872 | tf_op jit(solution)/shard_map/ppermute | solution.py:227
  20.2 13.7 %copy-start = (bf16[256,8192]{1,0:T(8,128)(2,1)S(1)}, bf16[256,8192]{1,0:T(8,128)(2,1)}, u32[]{:S(2)}) copy-start(bf16[256,8192]{1,0:T(8,128)(2,1)} %weight_ref.1) | copy-start | bytes 12582916

commit v6 on v5

--- a/solution.py
+++ b/solution.py
@@ -14,6 +14,8 @@
 CHIPS = 8
 D = 8192
 BLOCKS = D // 128
+PITCH = BLOCKS + 8
+QUERY_PITCH = HQ + 8
 WIDTH = 1024
 ROWS = 10
 SCALE = HEAD_SIZE ** (-0.5)
@@ -93,7 +95,8 @@
     out_ref,
     queries,
 ):
-    queries[...] = query_ref[...].reshape(CHIPS * HQ, 128).astype(F32)
+    for i in range(CHIPS):
+        queries[QUERY_PITCH * i : QUERY_PITCH * i + HQ] = query_ref[i].astype(F32)
     row = lax.broadcasted_iota(jnp.int32, (32, 128), 0)
     lane = lax.broadcasted_iota(jnp.int32, (32, 128), 1)
     mark = lane == row % 16 + 16 * (place_ref[0] // 2)
@@ -103,7 +106,7 @@
     parts = (prefix_ref, other_ref, own_ref)
     scores = []
     for k, head in enumerate(heads):
-        query = [queries[pl.ds(k * GROUP + g, 8, stride=HQ), :] for g in range(GROUP)]
+        query = [queries[pl.ds(k * GROUP + g, 8, stride=QUERY_PITCH), :] for g in range(GROUP)]
         query = jnp.concatenate(query, axis=0).astype(BF16)
         keys = jnp.concatenate([part[:128, head] for part in parts], axis=0)
         product = lax.dot_general(
@@ -172,10 +175,12 @@
         piece = jnp.dot(attn, weight_ref[:, n : n + WIDTH], preferred_element_type=F32)
         for i in range(WIDTH // 128):
             for c in range(2):
-                rows[pl.ds(c * BLOCKS + n // 128 + i, 8, stride=2 * BLOCKS), :] = piece[
+                rows[pl.ds(8 * PITCH * c + n // 128 + i, 8, stride=PITCH), :] = piece[
                     8 * c : 8 * c + 8, 128 * i : 128 * i + 128
                 ]
-    out_ref[...] = rows[...].astype(BF16).reshape(SAMPLES, BLOCKS, 128)
+    for b in range(SAMPLES):
+        at = PITCH * (8 * (b % 2) + b // 2)
+        out_ref[b] = rows[at : at + BLOCKS].astype(BF16)
 
 
 def finish_kernel(got_ref, residual_ref, gain_ref, hidden_ref, normed_ref):
@@ -253,7 +258,7 @@
         out_shape=jax.ShapeDtypeStruct((SAMPLES, ROWS, 2, 128), BF16),
         in_specs=smem(1) + vmem(5),
         out_specs=vmem(1)[0],
-        scratch_shapes=[pltpu.VMEM((CHIPS * HQ, 128), F32)],
+        scratch_shapes=[pltpu.VMEM((CHIPS * QUERY_PITCH, 128), F32)],
         compiler_params=at_most(8),
         cost_estimate=LONG,
     )(place, queries, prefix, other_prefix, own, bias)
@@ -263,7 +268,7 @@
         out_shape=jax.ShapeDtypeStruct((SAMPLES, BLOCKS, 128), BF16),
         in_specs=smem(1) + vmem(2),
         out_specs=vmem(1)[0],
-        scratch_shapes=[pltpu.VMEM((SAMPLES * BLOCKS, 128), F32)],
+        scratch_shapes=[pltpu.VMEM((SAMPLES * PITCH, 128), F32)],
         compiler_params=at_most(12),
         cost_estimate=LONG,
     )(place, partial, out_weight)

time: 50.5 us -> 50.4 us (level)
  no operation moved by 1% of the time
where the time goes in v6:
time: 50.4 us; the launch traced here: 50 us
  blocking collectives  27.1 us (54%)
  starting transfers between devices  13.8 us (27%)
  Pallas kernels  3.49 us (7%)
  waiting for transfers between devices  2.67 us (5%)
  between operations  2.1 us (4%)
  local copies, waits for them, and re-layouts  0.82 us (2%)
    all_to_all x1, blocking collectives, local(): proj = lax.all_to_all(proj, 'mp', 0, 0, tiled=True)  14.1 us
    all_to_all x1, blocking collectives, local(): partial = lax.all_to_all(partial, 'mp', 0, 0, tiled=True)  13 us
    all_to_all x1, starting transfers between devices, local(): lax.all_to_all(spread, 'mp', 0, 0, tiled=True, axis_index_groups=cores)  10.9 us
    ppermute x1, starting transfers between devices, local(): lax.ppermute(prefix, 'mp', [(i, i ^ 1) for i in range(SAMPLES)])  3 us
    all_to_all x1, waiting for transfers between devices, local(): lax.all_to_all(spread, 'mp', 0, 0, tiled=True, axis_index_groups=cores)  2.67 us
    pallas_call x1, Pallas kernels, local(): pl.pallas_call(project_kernel, out_shape=jax.ShapeDtypeStruct((SAMPLES, B...  1.2 us
  transfers between devices with their start and end apart: 2, of which 1 were waited for; matrix products, arithmetic and copies ran while one was open for 0% of the time, Pallas kernels for 0%

profile of v6, /device:TPU:1, one launch (start us, length us, event | category | flops | bytes accessed | tf_op | source)
XLA Modules:
  0.0 50.0 jit_solution(11165552925205028456)
XLA Ops:
  0.6 0.0 copy-start.2
  0.6 0.0 copy-start.1
  0.6 0.0 copy-start.6
  0.7 0.8 %copy-done.6 = bf16[1,4096]{1,0:T(2,128)(2,1)S(1)} copy-done((bf16[1,4096]{1,0:T(2,128)(2,1)S(1)}, bf16[1,4096]{1,0:T(2,128)(2,1)}, u32[]{:S(2)}) %copy-start.6) | copy-done | bytes 8216
  1.4 0.6 %shard_map.131 = bf16[8,32,128]{2,1,0:T(8,128)(2,1)} custom-call(bf16[1,4096]{1,0:T(2,128)(2,1)S(1)} %copy-done.6), custom_call_target="tpu_custom_call" | custom-call | flops 10000000000 | bytes 1000000 | tf_op jit(solution)/shard_map/pallas_call | solution.py:215
  2.1 10.9 %all-to-all-start = ((bf16[8,32,128]{2,1,0:T(8,128)(2,1)}), bf16[8,32,128]{2,1,0:T(8,128)(2,1)S(1)}, u32[]{:S(2)}, u32[]{:S(2)}) async-start(bf16[8,32,128]{2,1,0:T(8,128)(2,1)} %shard_map.131), calls=%async_computation | async-start | bytes 131072 | tf_op jit(solution)/shard_map/all_to_all | solution.py:223
  12.9 0.0 copy-done.2
  12.9 0.0 copy-done.1
  12.9 0.0 copy-start.3
  12.9 0.0 copy-start.4
  13.0 0.0 copy-start.5
  13.0 0.0 copy-start.7
  13.0 0.0 copy-start.8
  13.0 0.0 copy-start.9
  13.1 3.0 %collective-permute-start = (bf16[256,1024]{1,0:T(8,128)(2,1)S(1)}, bf16[256,1024]{1,0:T(8,128)(2,1)S(1)}, u32[]{:S(2)}, u32[]{:S(2)}) collective-permute-start(bf16[256,1024]{1,0:T(8,128)(2,1)S(1)} %shard_map.132.prefix_ref), channel_id=1, source_target_pairs={{0,1},{1,0},{2,3},{3,2},{4,5},{5,4},{6,7},{7,6},{8,9},{9,8},{10,11... | collective-permute-start | bytes 1572872 | tf_op jit(solution)/shard_map/ppermute | solution.py:232
  17.4 0.0 copy-done.3
  17.4 0.0 copy-done.4
  17.4 0.0 copy-done.5
  17.4 0.0 copy-done.7
  17.4 0.0 copy-done.8
  17.4 0.0 copy-done.9
  17.4 0.1 shard_map.133
  17.5 2.7 %all-to-all-done.query_ref = bf16[8,32,128]{2,1,0:T(8,128)(2,1)S(1)} async-done(((bf16[8,32,128]{2,1,0:T(8,128)(2,1)}), bf16[8,32,128]{2,1,0:T(8,128)(2,1)S(1)}, u32[]{:S(2)}, u32[]{:S(2)}) %all-to-all-start) | async-done | bytes 65568 | tf_op jit(solution)/shard_map/all_to_all | solution.py:223
  20.2 0.0 collective-permute-done.other_ref
  20.2 0.0 copy-start
  20.2 0.7 %shard_map.134 = bf16[16,10,2,128]{3,2,1,0:T(2,128)(2,1)S(1)} custom-call(s32[1]{0:T(128)} %bitcast.place_ref, bf16[8,32,128]{2,1,0:T(8,128)(2,1)S(1)} %all-to-all-done.query_ref, bf16[256,1024]{1,0:T(8,128)(2,1)S(1)} %shard_map.132.prefix_ref, bf16[256,1024]{1,0:T(8,128)(2,1)S(1)} %collective-permute-done.other_ref, ...), custom_call_target="tpu_custom_call" | custom-call | flops 10000000000 | bytes 1000000 | tf_op jit(solution)/shard_map/pallas_call | solution.py:256
  20.9 13.0 %all_to_all.15.got_ref = bf16[16,10,2,128]{3,2,1,0:T(2,128)(2,1)S(1)} all-to-all(bf16[16,10,2,128]{3,2,1,0:T(2,128)(2,1)S(1)} %shard_map.134), channel_id=1, replica_groups=mesh['dp'=32,'mp'=16] {'mp'}, dimensions={0} | all-to-all | bytes 163840 | tf_op jit(solution)/shard_map/all_to_all | solution.py:265
  33.9 0.0 copy-done
  33.9 1.2 %shard_map.135 = bf16[16,64,128]{2,1,0:T(8,128)(2,1)S(1)} custom-call(s32[1]{0:T(128)} %bitcast.place_ref, bf16[16,10,2,128]{3,2,1,0:T(2,128)(2,1)S(1)} %all_to_all.15.got_ref, bf16[256,8192]{1,0:T(8,128)(2,1)S(1)} %copy-done), custom_call_target="tpu_custom_call" | custom-call | flops 10000000000 | bytes 1000000 | tf_op jit(solution)/shard_map/pallas_call | solution.py:266
  35.1 14.1 %all_to_all.16.got_ref = bf16[16,64,128]{2,1,0:T(8,128)(2,1)S(1)} all-to-all(bf16[16,64,128]{2,1,0:T(8,128)(2,1)S(1)} %shard_map.135), channel_id=1, replica_groups=mesh['dp'=32,'mp'=16] {'mp'}, dimensions={0} | all-to-all | bytes 524288 | tf_op jit(solution)/shard_map/all_to_all | solution.py:275
  49.2 0.8 %shard_map.136 = (bf16[1,8192]{1,0:T(2,128)(2,1)}, bf16[1,8192]{1,0:T(2,128)(2,1)}) custom-call(bf16[16,64,128]{2,1,0:T(8,128)(2,1)S(1)} %all_to_all.16.got_ref, f32[64,128]{1,0:T(8,128)S(1)} %get-tuple-element.8.residual_ref, f32[64,128]{1,0:T(8,128)S(1)} %get-tuple-element.9.gain_ref), custom_call_target="tpu_custom_call" | custom-call | tf_op jit(solution)/shard_map/pallas_call | solution.py:277
  (1 shorter events, 0.0 us)
Async XLA Ops:
  0.6 12.3 %copy-start.2 = (bf16[128,1024]{1,0:T(8,128)(2,1)S(1)}, bf16[128,1024]{1,0:T(8,128)(2,1)}, u32[]{:S(2)}) copy-start(bf16[128,1024]{1,0:T(8,128)(2,1)} %pvalues_ref.1) | copy-start | bytes 786436
  0.6 12.3 %copy-start.1 = (bf16[128,1024]{1,0:T(8,128)(2,1)S(1)}, bf16[128,1024]{1,0:T(8,128)(2,1)}, u32[]{:S(2)}) copy-start(bf16[128,1024]{1,0:T(8,128)(2,1)} %pkeys_ref.1) | copy-start | bytes 786436
  0.6 0.8 %copy-start.6 = (bf16[1,4096]{1,0:T(2,128)(2,1)S(1)}, bf16[1,4096]{1,0:T(2,128)(2,1)}, u32[]{:S(2)}) copy-start(bf16[1,4096]{1,0:T(2,128)(2,1)} %query_ref.1) | copy-start | bytes 24580
  2.1 18.1 %all-to-all-start = ((bf16[8,32,128]{2,1,0:T(8,128)(2,1)}), bf16[8,32,128]{2,1,0:T(8,128)(2,1)S(1)}, u32[]{:S(2)}, u32[]{:S(2)}) async-start(bf16[8,32,128]{2,1,0:T(8,128)(2,1)} %shard_map.131), calls=%async_computation | async-start | bytes 131072 | tf_op jit(solution)/shard_map/all_to_all | solution.py:223
  12.9 4.4 %copy-start.3 = (bf16[1,64,1024]{2,1,0:T(8,128)(2,1)S(1)}, bf16[1,64,1024]{2,1,0:T(8,128)(2,1)}, u32[]{:S(2)}) copy-start(bf16[1,64,1024]{2,1,0:T(8,128)(2,1)} %skeys_ref.1) | copy-start | bytes 393220
  12.9 4.4 %copy-start.4 = (bf16[1,64,1024]{2,1,0:T(8,128)(2,1)S(1)}, bf16[1,64,1024]{2,1,0:T(8,128)(2,1)}, u32[]{:S(2)}) copy-start(bf16[1,64,1024]{2,1,0:T(8,128)(2,1)} %svalues_ref.1) | copy-start | bytes 393220
  13.0 4.4 %copy-start.5 = (bf16[1,8192]{1,0:T(2,128)(2,1)S(1)}, bf16[1,8192]{1,0:T(2,128)(2,1)}, u32[]{:S(2)}) copy-start(bf16[1,8192]{1,0:T(2,128)(2,1)} %residual_ref.1) | copy-start | bytes 49156
  13.0 4.4 %copy-start.7 = (bf16[8192]{0:T(1024)(128)(2,1)S(1)}, bf16[8192]{0:T(1024)(128)(2,1)}, u32[]{:S(2)}) copy-start(bf16[8192]{0:T(1024)(128)(2,1)} %param.23) | copy-start | bytes 49156
  13.0 4.4 %copy-start.8 = (bf16[1,1024]{1,0:T(2,128)(2,1)S(1)}, bf16[1,1024]{1,0:T(2,128)(2,1)}, u32[]{:S(2)}) copy-start(bf16[1,1024]{1,0:T(2,128)(2,1)} %key_ref.1) | copy-start | bytes 6148
  13.0 4.4 %copy-start.9 = (bf16[1,1024]{1,0:T(2,128)(2,1)S(1)}, bf16[1,1024]{1,0:T(2,128)(2,1)}, u32[]{:S(2)}) copy-start(bf16[1,1024]{1,0:T(2,128)(2,1)} %value_ref.1) | copy-start | bytes 6148
  13.1 7.1 %collective-permute-start = (bf16[256,1024]{1,0:T(8,128)(2,1)S(1)}, bf16[256,1024]{1,0:T(8,128)(2,1)S(1)}, u32[]{:S(2)}, u32[]{:S(2)}) collective-permute-start(bf16[256,1024]{1,0:T(8,128)(2,1)S(1)} %shard_map.132.prefix_ref), channel_id=1, source_target_pairs={{0,1},{1,0},{2,3},{3,2},{4,5},{5,4},{6,7},{7,6},{8,9},{9,8},{10,11... | collective-permute-start | bytes 1572872 | tf_op jit(solution)/shard_map/ppermute | solution.py:232
  20.2 13.7 %copy-start = (bf16[256,8192]{1,0:T(8,128)(2,1)S(1)}, bf16[256,8192]{1,0:T(8,128)(2,1)}, u32[]{:S(2)}) copy-start(bf16[256,8192]{1,0:T(8,128)(2,1)} %weight_ref.1) | copy-start | bytes 12582916
